TPU v7x, 32 devices: a whole 2x2x4 slice. The times are simulated.
32 devices in a mesh: rows: 16 (over z, x, core), cols: 2 (over y).
Axes of the slice: x: 2, y: 2, z: 4, core: 2. Of those that a mesh axis runs over, the one named last changes fastest.
Arguments:
- tokens: bfloat16 [32768, 1024], P('rows', 'cols'), may hold values from -6 to 6
- cotangent: bfloat16 [32768, 1024], P('rows', 'cols'), may hold values from -6 to 6
- first_gain: float32 [1024], replicated, may hold values from 0.5 to 1.5
- first_shift: float32 [1024], replicated, may hold values from -1.75 to 1.75
- second_gain: float32 [1024], replicated, may hold values from 0.5 to 1.5
- second_shift: float32 [1024], replicated, may hold values from -1.75 to 1.75
- query_weight: float32 [1024, 1024], P('rows', 'cols'), may hold values from -0.1875 to 0.1875
- key_weight: float32 [1024, 1024], P('rows', 'cols'), may hold values from -0.1875 to 0.1875
- value_weight: float32 [1024, 1024], P('rows', 'cols'), may hold values from -0.1875 to 0.1875
- query_bias: float32 [1024], P('cols'), may hold values from -3 to 3
- value_bias: float32 [1024], P('cols'), may hold values from -3 to 3
- output_weight: float32 [1024, 1024], P('cols', 'rows'), may hold values from -0.75 to 0.75
- up_weight: float32 [1024, 4096], P('rows', 'cols'), may hold values from -0.1875 to 0.1875
- up_bias: float32 [4096], P('cols'), may hold values from -3 to 3
- down_weight: float32 [4096, 1024], P('cols', 'rows'), may hold values from -0.09375 to 0.09375
- out_bias: float32 [1024], P('cols'), may hold values from -3 to 3
- first_gain_moment: float32 [1024], replicated, may hold values from -512 to 512
- first_shift_moment: float32 [1024], replicated, may hold values from -512 to 512
- second_gain_moment: float32 [1024], replicated, may hold values from -512 to 512
- second_shift_moment: float32 [1024], replicated, may hold values from -512 to 512
- query_moment: float32 [1024, 1024], P('rows', 'cols'), may hold values from -448 to 448
- key_moment: float32 [1024, 1024], P('rows', 'cols'), may hold values from -448 to 448
- value_moment: float32 [1024, 1024], P('rows', 'cols'), may hold values from -448 to 448
- query_bias_moment: float32 [1024], P('cols'), may hold values from -448 to 448
- value_bias_moment: float32 [1024], P('cols'), may hold values from -448 to 448
- output_moment: float32 [1024, 1024], P('cols', 'rows'), may hold values from -160 to 160
- up_moment: float32 [1024, 4096], P('rows', 'cols'), may hold values from -448 to 448
- up_bias_moment: float32 [4096], P('cols'), may hold values from -448 to 448
- down_moment: float32 [4096, 1024], P('cols', 'rows'), may hold values from -640 to 640
- out_bias_moment: float32 [1024], P('cols'), may hold values from -1024 to 1024
Outputs:
- result: bfloat16 [32768, 1024], P('rows', 'cols')
- tokens_grad: float32 [32768, 1024], P('rows', 'cols')
- first_gain_grad: float32 [1024], replicated
- first_shift_grad: float32 [1024], replicated
- second_gain_grad: float32 [1024], replicated
- second_shift_grad: float32 [1024], replicated
- query_weight_grad: float32 [1024, 1024], P('rows', 'cols')
- key_weight_grad: float32 [1024, 1024], P('rows', 'cols')
- value_weight_grad: float32 [1024, 1024], P('rows', 'cols')
- query_bias_grad: float32 [1024], P('cols')
- value_bias_grad: float32 [1024], P('cols')
- output_weight_grad: float32 [1024, 1024], P('cols', 'rows')
- up_weight_grad: float32 [1024, 4096], P('rows', 'cols')
- up_bias_grad: float32 [4096], P('cols')
- down_weight_grad: float32 [4096, 1024], P('cols', 'rows')
- out_bias_grad: float32 [1024], P('cols')
- first_gain_moment_new: float32 [1024], replicated
- first_shift_moment_new: float32 [1024], replicated
- second_gain_moment_new: float32 [1024], replicated
- second_shift_moment_new: float32 [1024], replicated
- query_moment_new: float32 [1024, 1024], P('rows', 'cols')
- key_moment_new: float32 [1024, 1024], P('rows', 'cols')
- value_moment_new: float32 [1024, 1024], P('rows', 'cols')
- query_bias_moment_new: float32 [1024], P('cols')
- value_bias_moment_new: float32 [1024], P('cols')
- output_moment_new: float32 [1024, 1024], P('cols', 'rows')
- up_moment_new: float32 [1024, 4096], P('rows', 'cols')
- up_bias_moment_new: float32 [4096], P('cols')
- down_moment_new: float32 [4096, 1024], P('cols', 'rows')
- out_bias_moment_new: float32 [1024], P('cols')
- first_gain_new: float32 [1024], replicated
- first_shift_new: float32 [1024], replicated
- second_gain_new: float32 [1024], replicated
- second_shift_new: float32 [1024], replicated
- query_weight_new: float32 [1024, 1024], P('rows', 'cols')
- key_weight_new: float32 [1024, 1024], P('rows', 'cols')
- value_weight_new: float32 [1024, 1024], P('rows', 'cols')
- query_bias_new: float32 [1024], P('cols')
- value_bias_new: float32 [1024], P('cols')
- output_weight_new: float32 [1024, 1024], P('cols', 'rows')
- up_weight_new: float32 [1024, 4096], P('rows', 'cols')
- up_bias_new: float32 [4096], P('cols')
- down_weight_new: float32 [4096, 1024], P('cols', 'rows')
- out_bias_new: float32 [1024], P('cols')
All inputs are finite; a program needn't handle non-finite values.
Results may differ from a plain program's by a relative error of at most 0.012.
The roundings to bfloat16 on the way count: a program that leaves them out, or rounds other values in their place, can miss the bound.
Values may be sent and summed in bfloat16 or wider, within the bound.
A program may use at most 256 MiB of HBM per device.

v0:
```python
from functools import partial
import math

import jax
import jax.numpy as jnp
from jax import lax
from jax.sharding import PartitionSpec as P

D = 1024
HD = 64
ROT = 16
FF = 4096
LEN = 1024
BLOCK = 512
ITERS = 5


EPSILON = 1e-05
NORM_FLOOR = 1e-07
COEF_FIRST = 3.4445
COEF_SECOND = -4.775
COEF_THIRD = 2.0315
MOMENTUM = 0.9
MATRIX_RATE = 0.5
VECTOR_RATE = 0.1
MASKED = -1000000000.0
HIGHEST = lax.Precision.HIGHEST


def low_product(left, right):
    return jnp.dot(left, right, preferred_element_type=jnp.float32)


def times_transpose(left, right):
    return lax.dot_general(
        left, right, (((1,), (1,)), ((), ())), preferred_element_type=jnp.float32
    )


def inner_rows(left, right):
    return lax.dot_general(
        left, right, (((0,), (0,)), ((), ())), preferred_element_type=jnp.float32
    )


def inner_high(left, right):
    return lax.dot_general(left, right, (((0,), (0,)), ((), ())), precision=HIGHEST)


def outer_high(left, right):
    return lax.dot_general(left, right, (((1,), (1,)), ((), ())), precision=HIGHEST)


def rotary_tables(row_count):
    half_width = ROT // 2
    frequency = jnp.power(10000.0, -jnp.arange(half_width, dtype=jnp.float32) * 2.0 / ROT)
    angles = (jnp.arange(row_count) % LEN).astype(jnp.float32)[:, None] * frequency[None, :]
    return (jnp.cos(angles)[:, None, :], jnp.sin(angles)[:, None, :])


def rotate(values, cosine, sine_table):
    half_width = ROT // 2
    first_half = values[..., :half_width]
    second_half = values[..., half_width:ROT]
    return jnp.concatenate(
        [
            first_half * cosine - second_half * sine_table,
            second_half * cosine + first_half * sine_table,
            values[..., ROT:],
        ],
        axis=-1,
    )


def block_scores(queries, key_heads, block_start):
    score_scale = 1.0 / math.sqrt(HD)
    scores = (
        jnp.einsum("qhd,khd->hqk", queries, key_heads, preferred_element_type=jnp.float32)
        * score_scale
    )
    query_place = block_start + jnp.arange(queries.shape[0])
    key_place = jnp.arange(key_heads.shape[0])
    allowed = key_place[None, :] <= query_place[:, None]
    return jnp.where(allowed[None], scores, MASKED)


def attend_forward(packed):
    queries, key_heads, values = packed
    outputs = []
    log_totals = []
    for block_index in range(LEN // BLOCK):
        start_row = block_index * BLOCK
        end_row = start_row + BLOCK
        scores = block_scores(queries[start_row:end_row], key_heads[:end_row], start_row)
        row_max = jnp.max(scores, axis=-1, keepdims=True)
        raw_weights = jnp.exp(scores - row_max)
        row_total = jnp.sum(raw_weights, axis=-1, keepdims=True)
        weights_low = (raw_weights / row_total).astype(jnp.bfloat16)
        outputs.append(
            jnp.einsum(
                "hqk,khd->qhd", weights_low, values[:end_row], preferred_element_type=jnp.float32
            )
        )
        log_totals.append(row_max + jnp.log(row_total))
    return (jnp.concatenate(outputs, 0), jnp.concatenate(log_totals, 1))


def attend_backward(packed):
    queries, key_heads, values, attended_back, log_totals = packed
    score_scale = 1.0 / math.sqrt(HD)
    query_parts = []
    key_back = jnp.zeros(key_heads.shape, jnp.float32)
    value_back = jnp.zeros(values.shape, jnp.float32)
    for block_index in range(LEN // BLOCK):
        start_row = block_index * BLOCK
        end_row = start_row + BLOCK
        query_block = queries[start_row:end_row]
        back_block = attended_back[start_row:end_row]
        scores = block_scores(query_block, key_heads[:end_row], start_row)
        softmax_weights = jnp.exp(scores - log_totals[:, start_row:end_row])
        weights_low = softmax_weights.astype(jnp.bfloat16)
        weights_back = jnp.einsum(
            "qhd,khd->hqk", back_block, values[:end_row], preferred_element_type=jnp.float32
        )
        row_delta = jnp.sum(softmax_weights * weights_back, axis=-1, keepdims=True)
        scores_back = (softmax_weights * (weights_back - row_delta)).astype(jnp.bfloat16)
        query_parts.append(
            jnp.einsum(
                "hqk,khd->qhd", scores_back, key_heads[:end_row], preferred_element_type=jnp.float32
            )
            * score_scale
        )
        key_part = (
            jnp.einsum("hqk,qhd->khd", scores_back, query_block, preferred_element_type=jnp.float32)
            * score_scale
        )
        value_part = jnp.einsum(
            "hqk,qhd->khd", weights_low, back_block, preferred_element_type=jnp.float32
        )
        padding = ((0, LEN - end_row), (0, 0), (0, 0))
        key_back = key_back + jnp.pad(key_part, padding)
        value_back = value_back + jnp.pad(value_part, padding)
    return (jnp.concatenate(query_parts, 0), key_back, value_back)


def shards(
    tokens,
    cotangent,
    first_gain,
    first_shift,
    second_gain,
    second_shift,
    query_weight,
    key_weight,
    value_weight,
    query_bias,
    value_bias,
    output_weight,
    up_weight,
    up_bias,
    down_weight,
    out_bias,
    first_gain_moment,
    first_shift_moment,
    second_gain_moment,
    second_shift_moment,
    query_moment,
    key_moment,
    value_moment,
    query_bias_moment,
    value_bias_moment,
    output_moment,
    up_moment,
    up_bias_moment,
    down_moment,
    out_bias_moment,
):
    row_devices = lax.axis_size("rows")
    row_count = tokens.shape[0]
    local_width = tokens.shape[1]
    hidden_width = up_bias.shape[0]
    head_count = local_width // HD
    whole_tokens, whole_cotangent = (
        lax.all_gather(tokens, "cols", axis=1, tiled=True),
        lax.all_gather(cotangent, "cols", axis=1, tiled=True),
    )
    query_full, key_full, value_full, up_full, output_full, down_full = (
        lax.all_gather(query_weight.astype(jnp.bfloat16), "rows", axis=0, tiled=True),
        lax.all_gather(key_weight.astype(jnp.bfloat16), "rows", axis=0, tiled=True),
        lax.all_gather(value_weight.astype(jnp.bfloat16), "rows", axis=0, tiled=True),
        lax.all_gather(up_weight.astype(jnp.bfloat16), "rows", axis=0, tiled=True),
        lax.all_gather(output_weight.astype(jnp.bfloat16), "rows", axis=1, tiled=True),
        lax.all_gather(down_weight.astype(jnp.bfloat16), "rows", axis=1, tiled=True),
    )
    tokens_f = whole_tokens.astype(jnp.float32)
    mean_value = jnp.mean(tokens_f, -1, keepdims=True)
    centered = tokens_f - mean_value
    inverse_scale = lax.rsqrt(jnp.mean(centered * centered, -1, keepdims=True) + EPSILON)
    normed = centered * inverse_scale
    first_input = (normed * first_gain + first_shift).astype(jnp.bfloat16)
    second_input = (normed * second_gain + second_shift).astype(jnp.bfloat16)
    projection = jnp.concatenate([query_full, key_full, value_full], axis=1)
    projected = low_product(first_input, projection)
    query_linear = projected[:, :local_width] + query_bias
    key_linear = projected[:, local_width : 2 * local_width]
    value_linear = projected[:, 2 * local_width :] + value_bias
    cosine, sine_table = rotary_tables(row_count)
    head_shape = (row_count, head_count, HD)
    sequence_shape = (row_count // LEN, LEN, head_count, HD)
    queries = (
        rotate(query_linear.reshape(head_shape), cosine, sine_table)
        .astype(jnp.bfloat16)
        .reshape(sequence_shape)
    )
    key_heads = (
        rotate(key_linear.reshape(head_shape), cosine, sine_table)
        .astype(jnp.bfloat16)
        .reshape(sequence_shape)
    )
    values = value_linear.astype(jnp.bfloat16).reshape(sequence_shape)
    attended, log_totals = lax.map(attend_forward, (queries, key_heads, values))
    attended_low = attended.reshape(row_count, local_width).astype(jnp.bfloat16)
    up_linear = low_product(second_input, up_full) + up_bias
    activation, activation_back = jax.vjp(partial(jax.nn.gelu, approximate=False), up_linear)
    hidden = activation.astype(jnp.bfloat16)
    branch = low_product(attended_low, output_full) + low_product(hidden, down_full)
    branch_share = lax.psum_scatter(branch, "cols", scatter_dimension=1, tiled=True)
    result = (tokens.astype(jnp.float32) + branch_share + out_bias).astype(jnp.bfloat16)
    attended_back = times_transpose(whole_cotangent, output_full).astype(jnp.bfloat16)
    hidden_back = times_transpose(whole_cotangent, down_full)
    up_back = activation_back(hidden_back)[0].astype(jnp.bfloat16)
    queries_back, keys_back, values_back = lax.map(
        attend_backward,
        (queries, key_heads, values, attended_back.reshape(sequence_shape), log_totals),
    )
    negative_sine = -sine_table
    query_back = (
        rotate(queries_back.reshape(head_shape), cosine, negative_sine)
        .reshape(row_count, local_width)
        .astype(jnp.bfloat16)
    )
    key_back = (
        rotate(keys_back.reshape(head_shape), cosine, negative_sine)
        .reshape(row_count, local_width)
        .astype(jnp.bfloat16)
    )
    value_back = values_back.reshape(row_count, local_width).astype(jnp.bfloat16)
    projected_back = jnp.concatenate([query_back, key_back, value_back], axis=1)
    first_back = times_transpose(projected_back, projection)
    second_back = times_transpose(up_back, up_full)
    norm_partials = jnp.stack(
        [
            jnp.sum(first_back * normed, 0),
            jnp.sum(first_back, 0),
            jnp.sum(second_back * normed, 0),
            jnp.sum(second_back, 0),
        ]
    )
    normed_back = lax.psum_scatter(
        first_back * first_gain + second_back * second_gain, "cols", scatter_dimension=1, tiled=True
    )
    own_normed = (tokens.astype(jnp.float32) - mean_value) * inverse_scale
    full_back = lax.all_gather(normed_back.astype(jnp.bfloat16), "cols", axis=1, tiled=True).astype(
        normed_back.dtype
    )
    back_mean = jnp.mean(full_back, -1, keepdims=True)
    cross_mean = jnp.mean(full_back * normed, -1, keepdims=True)
    tokens_grad = (
        cotangent.astype(jnp.float32)
        + (normed_back - back_mean - own_normed * cross_mean) * inverse_scale
    )
    weight_sums = lax.psum_scatter(
        jnp.concatenate(
            [
                inner_rows(first_input, projected_back),
                inner_rows(second_input, up_back),
                inner_rows(whole_cotangent, attended_low),
                inner_rows(whole_cotangent, hidden),
            ],
            axis=1,
        ),
        "rows",
        scatter_dimension=0,
        tiled=True,
    )
    query_weight_grad = weight_sums[:, :local_width]
    key_weight_grad = weight_sums[:, local_width : 2 * local_width]
    value_weight_grad = weight_sums[:, 2 * local_width : 3 * local_width]
    up_weight_grad = weight_sums[:, 3 * local_width : 3 * local_width + hidden_width]
    output_weight_grad = weight_sums[
        :, 3 * local_width + hidden_width : 4 * local_width + hidden_width
    ].T
    down_weight_grad = weight_sums[:, 4 * local_width + hidden_width :].T
    query_bias_grad, value_bias_grad, up_bias_grad, out_bias_grad = lax.psum(
        (
            jnp.sum(query_back, 0, dtype=jnp.float32),
            jnp.sum(value_back, 0, dtype=jnp.float32),
            jnp.sum(up_back, 0, dtype=jnp.float32),
            jnp.sum(cotangent, 0, dtype=jnp.float32),
        ),
        "rows",
    )
    query_moment_new = MOMENTUM * query_moment + query_weight_grad
    key_moment_new = MOMENTUM * key_moment + key_weight_grad
    value_moment_new = MOMENTUM * value_moment + value_weight_grad
    up_moment_new = MOMENTUM * up_moment + up_weight_grad
    output_moment_new = MOMENTUM * output_moment + output_weight_grad
    down_moment_new = MOMENTUM * down_moment + down_weight_grad
    oriented = (
        query_moment_new,
        key_moment_new,
        value_moment_new,
        up_moment_new,
        output_moment_new.T,
        down_moment_new.T,
    )
    squares = jnp.stack([jnp.sum(moment * moment) for moment in oriented])
    norm_totals, square_totals = lax.psum((norm_partials, squares), ("rows", "cols"))
    widths = [moment.shape[1] for moment in oriented]
    bounds = [sum(widths[:position]) for position in range(7)]
    packed = jnp.concatenate(
        [
            oriented[position] / (jnp.sqrt(square_totals[position]) + NORM_FLOOR)
            for position in range(6)
        ],
        axis=1,
    )
    for step_index in range(ITERS):
        gathered = lax.all_gather(packed, "rows", axis=0, tiled=True)
        gram_blocks = lax.psum(
            jnp.stack(
                [
                    outer_high(
                        gathered[:, bounds[position] : bounds[position + 1]],
                        packed[:, bounds[position] : bounds[position + 1]],
                    )
                    for position in range(6)
                ]
            ),
            "cols",
        )
        images = jnp.concatenate(
            [
                inner_high(
                    gram_blocks[position], gathered[:, bounds[position] : bounds[position + 1]]
                )
                for position in range(6)
            ],
            axis=1,
        )
        image_full = lax.all_gather(images, "rows", axis=0, tiled=True)
        seconds = jnp.concatenate(
            [
                inner_high(
                    gram_blocks[position], image_full[:, bounds[position] : bounds[position + 1]]
                )
                for position in range(6)
            ],
            axis=1,
        )
        packed = COEF_FIRST * packed + COEF_SECOND * images + COEF_THIRD * seconds
    orthogonal = [packed[:, bounds[position] : bounds[position + 1]] for position in range(6)]
    up_scale = math.sqrt(max(1.0, FF / D))
    query_weight_new = query_weight - MATRIX_RATE * orthogonal[0]
    key_weight_new = key_weight - MATRIX_RATE * orthogonal[1]
    value_weight_new = value_weight - MATRIX_RATE * orthogonal[2]
    up_weight_new = up_weight - MATRIX_RATE * (up_scale * orthogonal[3])
    output_weight_new = output_weight - MATRIX_RATE * orthogonal[4].T
    down_weight_new = down_weight - MATRIX_RATE * orthogonal[5].T
    vector_step = VECTOR_RATE / math.sqrt(row_count * row_devices)
    first_gain_grad = norm_totals[0]
    first_shift_grad = norm_totals[1]
    second_gain_grad = norm_totals[2]
    second_shift_grad = norm_totals[3]
    first_gain_moment_new = MOMENTUM * first_gain_moment + first_gain_grad
    first_shift_moment_new = MOMENTUM * first_shift_moment + first_shift_grad
    second_gain_moment_new = MOMENTUM * second_gain_moment + second_gain_grad
    second_shift_moment_new = MOMENTUM * second_shift_moment + second_shift_grad
    query_bias_moment_new = MOMENTUM * query_bias_moment + query_bias_grad
    value_bias_moment_new = MOMENTUM * value_bias_moment + value_bias_grad
    up_bias_moment_new = MOMENTUM * up_bias_moment + up_bias_grad
    out_bias_moment_new = MOMENTUM * out_bias_moment + out_bias_grad
    first_gain_new = first_gain - vector_step * first_gain_moment_new
    first_shift_new = first_shift - vector_step * first_shift_moment_new
    second_gain_new = second_gain - vector_step * second_gain_moment_new
    second_shift_new = second_shift - vector_step * second_shift_moment_new
    query_bias_new = query_bias - vector_step * query_bias_moment_new
    value_bias_new = value_bias - vector_step * value_bias_moment_new
    up_bias_new = up_bias - vector_step * up_bias_moment_new
    out_bias_new = out_bias - vector_step * out_bias_moment_new
    return (
        result,
        tokens_grad,
        first_gain_grad,
        first_shift_grad,
        second_gain_grad,
        second_shift_grad,
        query_weight_grad,
        key_weight_grad,
        value_weight_grad,
        query_bias_grad,
        value_bias_grad,
        output_weight_grad,
        up_weight_grad,
        up_bias_grad,
        down_weight_grad,
        out_bias_grad,
        first_gain_moment_new,
        first_shift_moment_new,
        second_gain_moment_new,
        second_shift_moment_new,
        query_moment_new,
        key_moment_new,
        value_moment_new,
        query_bias_moment_new,
        value_bias_moment_new,
        output_moment_new,
        up_moment_new,
        up_bias_moment_new,
        down_moment_new,
        out_bias_moment_new,
        first_gain_new,
        first_shift_new,
        second_gain_new,
        second_shift_new,
        query_weight_new,
        key_weight_new,
        value_weight_new,
        query_bias_new,
        value_bias_new,
        output_weight_new,
        up_weight_new,
        up_bias_new,
        down_weight_new,
        out_bias_new,
    )


def solution(mesh):
    in_specs = (
        P("rows", "cols"),
        P("rows", "cols"),
        P(),
        P(),
        P(),
        P(),
        P("rows", "cols"),
        P("rows", "cols"),
        P("rows", "cols"),
        P("cols"),
        P("cols"),
        P("cols", "rows"),
        P("rows", "cols"),
        P("cols"),
        P("cols", "rows"),
        P("cols"),
        P(),
        P(),
        P(),
        P(),
        P("rows", "cols"),
        P("rows", "cols"),
        P("rows", "cols"),
        P("cols"),
        P("cols"),
        P("cols", "rows"),
        P("rows", "cols"),
        P("cols"),
        P("cols", "rows"),
        P("cols"),
    )
    out_specs = (
        P("rows", "cols"),
        P("rows", "cols"),
        P(),
        P(),
        P(),
        P(),
        P("rows", "cols"),
        P("rows", "cols"),
        P("rows", "cols"),
        P("cols"),
        P("cols"),
        P("cols", "rows"),
        P("rows", "cols"),
        P("cols"),
        P("cols", "rows"),
        P("cols"),
        P(),
        P(),
        P(),
        P(),
        P("rows", "cols"),
        P("rows", "cols"),
        P("rows", "cols"),
        P("cols"),
        P("cols"),
        P("cols", "rows"),
        P("rows", "cols"),
        P("cols"),
        P("cols", "rows"),
        P("cols"),
        P(),
        P(),
        P(),
        P(),
        P("rows", "cols"),
        P("rows", "cols"),
        P("rows", "cols"),
        P("cols"),
        P("cols"),
        P("cols", "rows"),
        P("rows", "cols"),
        P("cols"),
        P("cols", "rows"),
        P("cols"),
    )
    return jax.shard_map(shards, mesh=mesh, in_specs=in_specs, out_specs=out_specs, check_vma=False)
```

profile of v0, /device:TPU:15, one launch (start us, length us, event | category | flops | bytes accessed | tf_op | source)
XLA Modules:
  0.0 3313.2 jit_solution(3645364824156739672)
XLA Ops:
  16.7 32.1 all-gather.22.cloned.1.call-done
  50.1 38.3 %all-gather.24.cloned.1.call-done = bf16[1024,512]{1,0:T(8,128)(2,1)} async-done(((bf16[64,512]{1,0:T(8,128)(2,1)}), bf16[1024,512]{1,0:T(8,128)(2,1)}) %all-gather.24.cloned.1.call-update) | async-done | bytes 1048592 | tf_op jit(solution)/shard_map/all_gather | solution.py:189
  89.7 38.3 %all-gather.26.cloned.1.call-done = bf16[1024,512]{1,0:T(8,128)(2,1)} async-done(((bf16[64,512]{1,0:T(8,128)(2,1)}), bf16[1024,512]{1,0:T(8,128)(2,1)}) %all-gather.26.cloned.1.call-update) | async-done | bytes 1048592 | tf_op jit(solution)/shard_map/all_gather | solution.py:190
  129.3 55.7 %all-gather.20.cloned.1.call-done = bf16[2048,1024]{1,0:T(8,128)(2,1)} async-done(((bf16[2048,512]{1,0:T(8,128)(2,1)}), bf16[2048,1024]{1,0:T(8,128)(2,1)}) %all-gather.20.cloned.1.call-update) | async-done | bytes 4194320 | tf_op jit(solution)/shard_map/all_gather | solution.py:184
  233.0 45.0 %while.28 = (s32[]{:T(128)}, bf16[2,1024,8,64]{1,3,2,0:T(8,128)(2,1)}, f32[2,8,1024,1]{2,1,3,0:T(8,128)S(1)}, bf16[2,1024,8,64]{1,3,2,0:T(8,128)(2,1)}, bf16[2,1...) while((s32[]{:T(128)}, ...), condition=%wide.region_7.8_spmd, body=%wide.region_2.7_spmd.sunk | while | flops 1688994304 | bytes 111483600 | solution.py:221
  302.1 306.2 %while.29 = (s32[]{:T(128)}, f32[2,1024,8,64]{1,0,3,2:T(2,128)}, f32[2,1024,8,64]{1,0,3,2:T(2,128)}, bf16[2,1024,8,64]{1,3,2,0:T(8,128)(2,1)}, bf16[2,1024,8,64]...) while((s32[]{:T(128)}, f32[2,1024,8,64]{1,0,3,2:T(2,128)}, ...), condition=%wide.region_12.13_spmd, body=%wide.region_9.12_spmd.sunk | while | flops 4099400192 | bytes 346827680 | solution.py:232
  355.3 36.7 %dynamic_update_slice.37 = f32[2,1024,8,64]{1,0,3,2:T(2,128)} dynamic-update-slice(f32[2,1024,8,64]{1,0,3,2:T(2,128)} %get-tuple-element.526, f32[1,1024,8,64]{1,0,3,2:T(1,128)} %copy.135, s32[]{:T(128)S(6)} %copy.157, s32[]{:T(128)} %constant.86.clone.1..sunk.1, s32[]{:T(128)} %constant.86.clone.1..sunk.1, s32[]{:T(128)} %constant.86.clone.1..sunk.1) | dynamic-update-slice | bytes 4194308 | tf_op jit(solution)/shard_map/while/body/jit(dynamic_update_index_in_dim)/dynamic_update_slice | solution.py:221
  404.4 36.4 %dynamic_update_slice.38 = f32[2,1024,8,64]{1,0,3,2:T(2,128)} dynamic-update-slice(f32[2,1024,8,64]{1,0,3,2:T(2,128)} %get-tuple-element.527, f32[1,1024,8,64]{1,0,3,2:T(1,128)} %copy.136, s32[]{:T(128)S(6)} %copy.157, s32[]{:T(128)} %constant.86.clone.1..sunk.1, s32[]{:T(128)} %constant.86.clone.1..sunk.1, s32[]{:T(128)} %constant.86.clone.1..sunk.1) | dynamic-update-slice | bytes 4194308 | tf_op jit(solution)/shard_map/while/body/jit(dynamic_update_index_in_dim)/dynamic_update_slice | solution.py:221
  507.7 36.7 %dynamic_update_slice.37 = f32[2,1024,8,64]{1,0,3,2:T(2,128)} dynamic-update-slice(f32[2,1024,8,64]{1,0,3,2:T(2,128)} %get-tuple-element.526, f32[1,1024,8,64]{1,0,3,2:T(1,128)} %copy.135, s32[]{:T(128)S(6)} %copy.157, s32[]{:T(128)} %constant.86.clone.1..sunk.1, s32[]{:T(128)} %constant.86.clone.1..sunk.1, s32[]{:T(128)} %constant.86.clone.1..sunk.1) | dynamic-update-slice | bytes 4194308 | tf_op jit(solution)/shard_map/while/body/jit(dynamic_update_index_in_dim)/dynamic_update_slice | solution.py:221
  556.8 36.4 %dynamic_update_slice.38 = f32[2,1024,8,64]{1,0,3,2:T(2,128)} dynamic-update-slice(f32[2,1024,8,64]{1,0,3,2:T(2,128)} %get-tuple-element.527, f32[1,1024,8,64]{1,0,3,2:T(1,128)} %copy.136, s32[]{:T(128)S(6)} %copy.157, s32[]{:T(128)} %constant.86.clone.1..sunk.1, s32[]{:T(128)} %constant.86.clone.1..sunk.1, s32[]{:T(128)} %constant.86.clone.1..sunk.1) | dynamic-update-slice | bytes 4194308 | tf_op jit(solution)/shard_map/while/body/jit(dynamic_update_index_in_dim)/dynamic_update_slice | solution.py:221
  644.6 51.2 %multiply_convert_fusion.2 = (bf16[2048,2048]{1,0:T(8,128)(2,1)}, f32[2048,2048]{1,0:T(8,128)}, f32[2048,2048]{1,0:T(8,128)}) fusion(f32[2048]{0:T(1024)S(1)} %copy-done.102, bf16[1024,2048]{1,0:T(8,128)(2,1)} %all-gather.30.cloned.1.call-done, bf16[2048,1024]{1,0:T(8,128)(2,1)} %all-gather.20.cloned.1.call-done, f32[1024]{0:T(1024)S(1)} %copy-done.118, ...), kind=kOutput, calls=%fused_computation.102 | convolution fusion | flops 8879341568 | bytes 50364416 | tf_op jit(solution)/shard_map/dot_general | solution.py:31
  695.8 28.0 convert_reduce_fusion
  764.0 77.5 %reduce-scatter.6.cloned.1.call-done = f32[2048,512]{1,0:T(8,128)} async-done(((f32[2048,1024]{1,0:T(8,128)}), f32[2048,512]{1,0:T(8,128)}) %reduce-scatter.6.cloned.1.call-update) | async-done | bytes 4194320 | tf_op jit(solution)/shard_map/reduce_scatter | solution.py:259
  913.5 235.5 %reduce-scatter.8.cloned.1.call-done = f32[64,6144]{1,0:T(8,128)} async-done(((f32[1024,6144]{1,0:T(8,128)}), f32[64,6144]{1,0:T(8,128)}) %reduce-scatter.8.cloned.1.call-update) | async-done | bytes 1572880 | tf_op jit(solution)/shard_map/reduce_scatter | solution.py:272
  1160.0 40.9 %all-reduce.2 = (f32[4,1024]{1,0:T(4,128)}, f32[6]{0:T(128)S(1)}) all-reduce(f32[4,1024]{1,0:T(4,128)S(1)} %pad_maximum_fusion.7, f32[6]{0:T(128)S(1)} %stack.152), channel_id=1, replica_groups=mesh['rows'=16,'cols'=2] {'rows','cols'}, use_global_device_ids=true, to_apply=%region_20.21 | all-reduce | flops 4102 | bytes 32816 | tf_op jit(solution)/shard_map/psum | solution.py:318
  1207.1 129.6 %all-gather.38.cloned.1.call-done = f32[1024,6144]{1,0:T(8,128)} async-done(((f32[64,6144]{1,0:T(8,128)}), f32[1024,6144]{1,0:T(8,128)}) %all-gather.38.cloned.1.call-update) | async-done | bytes 25165840 | tf_op jit(solution)/shard_map/all_gather | solution.py:329
  1374.5 50.4 %all-reduce.10.cloned.1.call-done = f32[6,1024,64]{1,2,0:T(8,128)} async-done(((f32[6,1024,64]{1,2,0:T(8,128)}), f32[6,1024,64]{1,2,0:T(8,128)}) %all-reduce.10.cloned.1.call-update) | async-done | bytes 1572880 | tf_op jit(solution)/shard_map/psum | solution.py:330
  1453.5 129.9 %all-gather.40.cloned.1.call-done = f32[1024,6144]{1,0:T(8,128)} async-done(((f32[64,6144]{1,0:T(8,128)}), f32[1024,6144]{1,0:T(8,128)}) %all-gather.40.cloned.1.call-update) | async-done | bytes 25165840 | tf_op jit(solution)/shard_map/all_gather | solution.py:351
  1612.3 128.6 %all-gather.42.cloned.1.call-done = f32[1024,6144]{1,0:T(8,128)} async-done(((f32[64,6144]{1,0:T(8,128)}), f32[1024,6144]{1,0:T(8,128)}) %all-gather.42.cloned.1.call-update) | async-done | bytes 25165840 | tf_op jit(solution)/shard_map/all_gather | solution.py:329
  1778.5 50.4 %all-reduce.12.cloned.1.call-done = f32[6,1024,64]{1,2,0:T(8,128)} async-done(((f32[6,1024,64]{1,2,0:T(8,128)}), f32[6,1024,64]{1,2,0:T(8,128)}) %all-reduce.12.cloned.1.call-update) | async-done | bytes 1572880 | tf_op jit(solution)/shard_map/psum | solution.py:330
  1857.5 129.9 %all-gather.44.cloned.1.call-done = f32[1024,6144]{1,0:T(8,128)} async-done(((f32[64,6144]{1,0:T(8,128)}), f32[1024,6144]{1,0:T(8,128)}) %all-gather.44.cloned.1.call-update) | async-done | bytes 25165840 | tf_op jit(solution)/shard_map/all_gather | solution.py:351
  2016.3 128.6 %all-gather.46.cloned.1.call-done = f32[1024,6144]{1,0:T(8,128)} async-done(((f32[64,6144]{1,0:T(8,128)}), f32[1024,6144]{1,0:T(8,128)}) %all-gather.46.cloned.1.call-update) | async-done | bytes 25165840 | tf_op jit(solution)/shard_map/all_gather | solution.py:329
  2182.6 50.4 %all-reduce.14.cloned.1.call-done = f32[6,1024,64]{1,2,0:T(8,128)} async-done(((f32[6,1024,64]{1,2,0:T(8,128)}), f32[6,1024,64]{1,2,0:T(8,128)}) %all-reduce.14.cloned.1.call-update) | async-done | bytes 1572880 | tf_op jit(solution)/shard_map/psum | solution.py:330
  2261.5 129.8 %all-gather.48.cloned.1.call-done = f32[1024,6144]{1,0:T(8,128)} async-done(((f32[64,6144]{1,0:T(8,128)}), f32[1024,6144]{1,0:T(8,128)}) %all-gather.48.cloned.1.call-update) | async-done | bytes 25165840 | tf_op jit(solution)/shard_map/all_gather | solution.py:351
  2420.4 128.6 %all-gather.50.cloned.1.call-done = f32[1024,6144]{1,0:T(8,128)} async-done(((f32[64,6144]{1,0:T(8,128)}), f32[1024,6144]{1,0:T(8,128)}) %all-gather.50.cloned.1.call-update) | async-done | bytes 25165840 | tf_op jit(solution)/shard_map/all_gather | solution.py:329
  2586.6 50.4 %all-reduce.16.cloned.1.call-done = f32[6,1024,64]{1,2,0:T(8,128)} async-done(((f32[6,1024,64]{1,2,0:T(8,128)}), f32[6,1024,64]{1,2,0:T(8,128)}) %all-reduce.16.cloned.1.call-update) | async-done | bytes 1572880 | tf_op jit(solution)/shard_map/psum | solution.py:330
  2665.6 129.8 %all-gather.52.cloned.1.call-done = f32[1024,6144]{1,0:T(8,128)} async-done(((f32[64,6144]{1,0:T(8,128)}), f32[1024,6144]{1,0:T(8,128)}) %all-gather.52.cloned.1.call-update) | async-done | bytes 25165840 | tf_op jit(solution)/shard_map/all_gather | solution.py:351
  2824.4 128.6 %all-gather.54.cloned.1.call-done = f32[1024,6144]{1,0:T(8,128)} async-done(((f32[64,6144]{1,0:T(8,128)}), f32[1024,6144]{1,0:T(8,128)}) %all-gather.54.cloned.1.call-update) | async-done | bytes 25165840 | tf_op jit(solution)/shard_map/all_gather | solution.py:329
  3009.3 31.8 all-reduce.18.cloned.1.call-done
  3072.3 70.3 %reduce-scatter.4.cloned.1.call-done = f32[2048,512]{1,0:T(8,128)} async-done(((f32[2048,1024]{1,0:T(8,128)}), f32[2048,512]{1,0:T(8,128)}) %reduce-scatter.4.cloned.1.call-update) | async-done | bytes 4194320 | tf_op jit(solution)/shard_map/reduce_scatter | solution.py:227
  3150.2 47.1 %all-reduce.3 = (f32[512]{0:T(512)S(1)}, f32[512]{0:T(512)S(1)}, f32[2048]{0:T(1024)S(1)}, f32[512]{0:T(512)S(1)}) all-reduce(f32[512]{0:T(512)S(1)} %reduce_sum.217, f32[512]{0:T(512)S(1)} %reduce_sum.219, f32[2048]{0:T(1024)S(1)} %copy-done.106, f32[512]{0:T(512)S(1)} %get-tuple-element.332), channel_id=1, replica_groups=mesh['rows'=16,'cols'=2] {'rows'}, use_global_device_ids=true, to_apply=%region_23.24 | all-reduce | flops 3584 | bytes 28672 | tf_op jit(solution)/shard_map/psum | solution.py:294
  3201.0 73.5 %all-gather.56.cloned.1.call-done = f32[1024,6144]{1,0:T(8,128)} async-done(((f32[64,6144]{1,0:T(8,128)}), f32[1024,6144]{1,0:T(8,128)}) %all-gather.56.cloned.1.call-update) | async-done | bytes 25165840 | tf_op jit(solution)/shard_map/all_gather | solution.py:351
  (593 shorter events, 959.5 us)
Async XLA Ops:
  7.2 41.5 %all-gather.22.cloned.1.call-start = ((), (), s32[]{:S(2)}) async-start(), calls=%async_computation.4 | async-start | bytes 1114112 | tf_op jit(solution)/shard_map/all_gather | solution.py:188
  8.9 79.5 %all-gather.24.cloned.1.call-start = ((), (), s32[]{:S(2)}) async-start(), calls=%async_computation.5 | async-start | bytes 1114112 | tf_op jit(solution)/shard_map/all_gather | solution.py:189
  10.5 117.4 %all-gather.26.cloned.1.call-start = ((), (), s32[]{:S(2)}) async-start(), calls=%async_computation.6 | async-start | bytes 1114112 | tf_op jit(solution)/shard_map/all_gather | solution.py:190
  12.1 172.8 %all-gather.20.cloned.1.call-start = ((), (), s32[]{:S(2)}) async-start(), calls=%async_computation.3 | async-start | bytes 6291456 | tf_op jit(solution)/shard_map/all_gather | solution.py:184
  12.7 265.3 %all-gather.28.cloned.1.call-start = ((), (), s32[]{:S(2)}) async-start(), calls=%async_computation.7 | async-start | bytes 1114112 | tf_op jit(solution)/shard_map/all_gather | solution.py:192
  13.4 269.1 %all-gather.34.cloned.1.call-start = ((), (), s32[]{:S(2)}) async-start(), calls=%async_computation.11 | async-start | bytes 6291456 | tf_op jit(solution)/shard_map/all_gather | solution.py:185
  14.0 630.5 %all-gather.30.cloned.1.call-start = ((), (), s32[]{:S(2)}) async-start(), calls=%async_computation.8 | async-start | bytes 4456448 | tf_op jit(solution)/shard_map/all_gather | solution.py:191
  14.8 681.0 %all-gather.32.cloned.1.call-start = ((), (), s32[]{:S(2)}) async-start(), calls=%async_computation.9 | async-start | bytes 4456448 | tf_op jit(solution)/shard_map/all_gather | solution.py:193
  15.7 825.8 %reduce-scatter.6.cloned.1.call-start = ((), (), s32[]{:S(2)}) async-start(), calls=%async_computation.12 | async-start | bytes 12582912 | tf_op jit(solution)/shard_map/reduce_scatter | solution.py:259
  742.1 160.1 %all-gather.36.cloned.1.call-start = ((), (), s32[]{:S(2)}) async-start(), calls=%async_computation.13 | async-start | bytes 6291456 | tf_op jit(solution)/shard_map/all_gather | solution.py:263
  845.3 303.8 %reduce-scatter.8.cloned.1.call-start = ((), (), s32[]{:S(2)}) async-start(), calls=%async_computation.14 | async-start | bytes 26738688 | tf_op jit(solution)/shard_map/reduce_scatter | solution.py:272
  881.9 454.8 %all-gather.38.cloned.1.call-start = ((), (), s32[]{:S(2)}) async-start(), calls=%async_computation.15 | async-start | bytes 26738688 | tf_op jit(solution)/shard_map/all_gather | solution.py:329
  902.2 246.8 %copy-start.71 = (f32[64,2048]{1,0:T(8,128)S(1)}, f32[64,2048]{1,0:T(8,128)}, u32[]{:S(2)}) copy-start(f32[64,2048]{1,0:T(8,128)} %param.60) | copy-start | bytes 1572868
  902.2 249.5 %copy-start.83 = (f32[512,64]{0,1:T(8,128)S(1)}, f32[512,64]{0,1:T(8,128)}, u32[]{:S(2)}) copy-start(f32[512,64]{0,1:T(8,128)} %param.59) | copy-start | bytes 393220
  913.5 239.6 %copy-start.72 = (f32[2048,64]{0,1:T(8,128)S(1)}, f32[2048,64]{0,1:T(8,128)}, u32[]{:S(2)}) copy-start(f32[2048,64]{0,1:T(8,128)} %param.62) | copy-start | bytes 1572868
  1153.1 205.8 %copy-start.63 = (f32[512,64]{0,1:T(8,128)}, f32[512,64]{0,1:T(8,128)S(1)}, u32[]{:S(2)}) copy-start(f32[512,64]{0,1:T(8,128)S(1)} %get-tuple-element.293) | copy-start | bytes 393220
  1154.6 208.1 %copy-start.46 = (f32[2048,64]{0,1:T(8,128)}, f32[2048,64]{0,1:T(8,128)S(1)}, u32[]{:S(2)}) copy-start(f32[2048,64]{0,1:T(8,128)S(1)} %get-tuple-element.290) | copy-start | bytes 1572868
  1207.0 217.9 %all-reduce.10.cloned.1.call-start = ((), (), s32[]{:S(2)}) async-start(), calls=%async_computation.16 | async-start | bytes 3145728 | tf_op jit(solution)/shard_map/psum | solution.py:330
  1374.5 208.9 %all-gather.40.cloned.1.call-start = ((), (), s32[]{:S(2)}) async-start(), calls=%async_computation.17 | async-start | bytes 26738688 | tf_op jit(solution)/shard_map/all_gather | solution.py:351
  1453.5 287.5 %all-gather.42.cloned.1.call-start = ((), (), s32[]{:S(2)}) async-start(), calls=%async_computation.18 | async-start | bytes 26738688 | tf_op jit(solution)/shard_map/all_gather | solution.py:329
  1612.3 216.6 %all-reduce.12.cloned.1.call-start = ((), (), s32[]{:S(2)}) async-start(), calls=%async_computation.19 | async-start | bytes 3145728 | tf_op jit(solution)/shard_map/psum | solution.py:330
  1778.5 208.9 %all-gather.44.cloned.1.call-start = ((), (), s32[]{:S(2)}) async-start(), calls=%async_computation.20 | async-start | bytes 26738688 | tf_op jit(solution)/shard_map/all_gather | solution.py:351
  1857.4 287.5 %all-gather.46.cloned.1.call-start = ((), (), s32[]{:S(2)}) async-start(), calls=%async_computation.21 | async-start | bytes 26738688 | tf_op jit(solution)/shard_map/all_gather | solution.py:329
  2016.3 216.7 %all-reduce.14.cloned.1.call-start = ((), (), s32[]{:S(2)}) async-start(), calls=%async_computation.22 | async-start | bytes 3145728 | tf_op jit(solution)/shard_map/psum | solution.py:330
  2182.5 208.9 %all-gather.48.cloned.1.call-start = ((), (), s32[]{:S(2)}) async-start(), calls=%async_computation.23 | async-start | bytes 26738688 | tf_op jit(solution)/shard_map/all_gather | solution.py:351
  2261.5 287.5 %all-gather.50.cloned.1.call-start = ((), (), s32[]{:S(2)}) async-start(), calls=%async_computation.24 | async-start | bytes 26738688 | tf_op jit(solution)/shard_map/all_gather | solution.py:329
  2420.3 216.7 %all-reduce.16.cloned.1.call-start = ((), (), s32[]{:S(2)}) async-start(), calls=%async_computation.25 | async-start | bytes 3145728 | tf_op jit(solution)/shard_map/psum | solution.py:330
  2586.6 208.9 %all-gather.52.cloned.1.call-start = ((), (), s32[]{:S(2)}) async-start(), calls=%async_computation.26 | async-start | bytes 26738688 | tf_op jit(solution)/shard_map/all_gather | solution.py:351
  2665.5 287.5 %all-gather.54.cloned.1.call-start = ((), (), s32[]{:S(2)}) async-start(), calls=%async_computation.27 | async-start | bytes 26738688 | tf_op jit(solution)/shard_map/all_gather | solution.py:329
  2824.4 216.7 %all-reduce.18.cloned.1.call-start = ((), (), s32[]{:S(2)}) async-start(), calls=%async_computation.28 | async-start | bytes 3145728 | tf_op jit(solution)/shard_map/psum | solution.py:330
  2990.6 151.9 %reduce-scatter.4.cloned.1.call-start = ((), (), s32[]{:S(2)}) async-start(), calls=%async_computation.10 | async-start | bytes 12582912 | tf_op jit(solution)/shard_map/reduce_scatter | solution.py:227
  3009.2 265.3 %all-gather.56.cloned.1.call-start = ((), (), s32[]{:S(2)}) async-start(), calls=%async_computation.29 | async-start | bytes 26738688 | tf_op jit(solution)/shard_map/all_gather | solution.py:351
  (136 other events, 4321.4 us)
Sparse Core Ops, SparseCore 0:
  10.8 37.9 all-gather.21
  51.5 36.8 all-gather.23
  91.1 36.8 all-gather.25
  129.3 55.5 all-gather.19
  187.5 37.9 all-gather.27
  226.9 55.5 all-gather.33
  285.3 51.0 all-gather.29
  339.0 48.9 all-gather.31
  742.2 99.2 reduce-scatter.5
  845.4 56.7 all-gather.35
  906.3 242.6 reduce-scatter.7
  1207.2 129.5 all-gather.37
  1374.6 50.2 all-reduce.9
  1453.6 129.7 all-gather.39
  1612.4 128.5 all-gather.41
  1778.6 50.2 all-reduce.11
  1857.6 129.7 all-gather.43
  2016.4 128.5 all-gather.45
  2182.6 50.2 all-reduce.13
  2261.6 129.7 all-gather.47
  2420.5 128.5 all-gather.49
  2586.7 50.2 all-reduce.15
  2665.6 129.7 all-gather.51
  2824.5 128.5 all-gather.53
  2990.7 50.2 all-reduce.17
  3043.2 99.3 reduce-scatter.3
  3144.0 130.4 all-gather.55
where the time goes:
time: 3340 us; the launch traced here: 3310 us
  waiting for transfers between devices  2040 us (61%)
  matrix products  771 us (23%)
  local copies, waits for them, and re-layouts  260 us (8%)
  other arithmetic  127 us (4%)
  blocking collectives  87.9 us (3%)
    all_gather x5, waiting for transfers between devices, shards(): gathered = lax.all_gather(packed, 'rows', axis=0, tiled=True)  644 us
    all_gather x5, waiting for transfers between devices, shards(): image_full = lax.all_gather(images, 'rows', axis=0, tiled=True)  593 us
    dot_general x60, matrix products, inner_high(): lax.dot_general(left, right, (((0,), (0,)), ((), ())), precision=HIGHEST)  274 us
    reduce_scatter x1, waiting for transfers between devices, shards(): lax.psum_scatter(jnp.concatenate([inner_rows(first_input, projected_back)...  236 us
    psum x5, waiting for transfers between devices, shards(): lax.psum(jnp.stack([outer_high(gathered[:, bounds[position]:bounds[positi...  233 us
    dot_general x30, matrix products, outer_high(): lax.dot_general(left, right, (((1,), (1,)), ((), ())), precision=HIGHEST)  182 us
    dynamic_update_slice x8, local copies, waits for them, and re-layouts, shards(): attended, log_totals = lax.map(attend_forward, (queries, key_heads, values))  160 us
    reduce_scatter x1, waiting for transfers between devices, shards(): lax.psum_scatter(first_back * first_gain + second_back * second_gain, 'co...  77.5 us
  transfers between devices with their start and end apart: 27, of which 24 were waited for; matrix products, arithmetic and copies ran while one was open for 19% of the time, Pallas kernels for 0%

commit v1 on v0

v1 whole, which is shorter than its diff:
```python
from functools import partial
import math

import jax
import jax.numpy as jnp
from jax import lax
from jax.experimental import pallas as pl
from jax.experimental.pallas import tpu as pltpu
from jax.sharding import PartitionSpec as P

D = 1024
HD = 64
ROT = 16
FF = 4096
LEN = 1024
ITERS = 5

EPSILON = 1e-05
NORM_FLOOR = 1e-07
COEF_FIRST = 3.4445
COEF_SECOND = -4.775
COEF_THIRD = 2.0315
MOMENTUM = 0.9
MATRIX_RATE = 0.5
VECTOR_RATE = 0.1
MASKED = -1000000000.0
PAIR = 2 * HD
ROWS_STEP = 256
MESH = pl.DeviceIdType.MESH
F32 = jnp.float32
BF16 = jnp.bfloat16

OWNERS = ((1, 1), (6, 0), (4, 1), (2, 0), (3, 0), (5, 1))


def low_product(left, right):
    return jnp.dot(left, right, preferred_element_type=F32)


def times_transpose(left, right):
    return lax.dot_general(left, right, (((1,), (1,)), ((), ())), preferred_element_type=F32)


def inner_rows(left, right):
    return lax.dot_general(left, right, (((0,), (0,)), ((), ())), preferred_element_type=F32)


def three_pass(left, right):
    return jnp.dot(left, right, precision=lax.Precision.HIGH)


def rotary_tables():
    half = ROT // 2
    lane = jnp.arange(PAIR) % HD
    frequency = jnp.power(10000.0, -(lane % half).astype(F32) * 2.0 / ROT)
    angles = jnp.arange(LEN).astype(F32)[:, None] * frequency[None, :]
    cosine, sine = jnp.cos(angles), jnp.sin(angles)
    keep = jnp.where(lane < ROT, cosine, 1.0)
    ahead = jnp.where(lane < half, -sine, 0.0)
    behind = jnp.where((lane >= half) & (lane < ROT), sine, 0.0)
    return keep, ahead, behind


def attention_kernel(
    query_ref, key_ref, value_ref, back_ref, keep_ref, ahead_ref, behind_ref,
    out_ref, query_back_ref, key_back_ref, value_back_ref,
    queries, keys, values, query_sum, key_sum, value_sum, out_sum,
):
    half = ROT // 2
    scale = 1.0 / math.sqrt(HD)
    keep, ahead, behind = keep_ref[...], ahead_ref[...], behind_ref[...]

    def rotated(x, sign):
        up = pltpu.roll(x, PAIR - half, 1)
        down = pltpu.roll(x, half, 1)
        return x * keep + sign * (up * ahead + down * behind)

    queries[...] = (rotated(query_ref[...], 1.0).astype(BF16).astype(F32) * scale).astype(BF16)
    keys[...] = rotated(key_ref[...], 1.0).astype(BF16)
    values[...] = value_ref[...].astype(BF16)
    key_sum[...] = jnp.zeros_like(key_sum)
    value_sum[...] = jnp.zeros_like(value_sum)
    query_sum[...] = jnp.zeros_like(query_sum)
    out_sum[...] = jnp.zeros_like(out_sum)
    step = ROWS_STEP
    lower = lax.broadcasted_iota(jnp.int32, (step, step), 1) <= lax.broadcasted_iota(
        jnp.int32, (step, step), 0
    )
    lanes = lax.broadcasted_iota(jnp.int32, (step, PAIR), 1) // HD

    def head(place, carry):
        mine = lanes == place
        for block in range(LEN // step):
            rows = slice(block * step, (block + 1) * step)
            width = (block + 1) * step
            query = jnp.where(mine, queries[rows, :], 0).astype(BF16)
            back = jnp.where(mine, back_ref[rows, :], 0).astype(BF16)
            scores = times_transpose(query, keys[:width, :])
            last = jnp.where(lower, scores[:, width - step :], MASKED)
            if block:
                scores = jnp.concatenate([scores[:, : width - step], last], axis=1)
            else:
                scores = last
            raised = jnp.exp(scores - jnp.max(scores, axis=1, keepdims=True))
            probs = raised * (1.0 / jnp.sum(raised, axis=1, keepdims=True))
            probs_low = probs.astype(BF16)
            probs_back = times_transpose(back, values[:width, :])
            delta = jnp.sum(probs * probs_back, axis=1, keepdims=True)
            scores_back = (probs * (probs_back - delta)).astype(BF16)
            out_sum[rows, :] += jnp.where(mine, low_product(probs_low, values[:width, :]), 0.0)
            query_sum[rows, :] += jnp.where(mine, low_product(scores_back, keys[:width, :]), 0.0)
            key_sum[:width, :] += inner_rows(scores_back, query)
            value_sum[:width, :] += inner_rows(probs_low, back)
        return carry

    lax.fori_loop(0, PAIR // HD, head, 0)
    out_ref[...] = out_sum[...].astype(BF16)
    query_back_ref[...] = rotated(query_sum[...] * scale, -1.0).astype(BF16)
    key_back_ref[...] = rotated(key_sum[...], -1.0).astype(BF16)
    value_back_ref[...] = value_sum[...].astype(BF16)


def attention(projected, attended_back, tables):
    rows, width = attended_back.shape
    pairs = width // PAIR
    piece = (LEN, PAIR)
    table = pl.BlockSpec(piece, lambda s, p: (0, 0), pipeline_mode=pl.Buffered(1))
    plain = pl.BlockSpec(piece, lambda s, p: (s, p))
    shape = jax.ShapeDtypeStruct((rows, width), BF16)
    products = 6 * rows * LEN * PAIR * pairs * 2
    return pl.pallas_call(
        attention_kernel,
        grid=(rows // LEN, pairs),
        in_specs=[
            plain,
            pl.BlockSpec(piece, lambda s, p: (s, pairs + p)),
            pl.BlockSpec(piece, lambda s, p: (s, 2 * pairs + p)),
            plain,
            table,
            table,
            table,
        ],
        out_specs=[plain] * 4,
        out_shape=[shape] * 4,
        scratch_shapes=[pltpu.VMEM(piece, BF16)] * 3 + [pltpu.VMEM(piece, F32)] * 4,
        compiler_params=pltpu.CompilerParams(vmem_limit_bytes=40 << 20),
        cost_estimate=pl.CostEstimate(
            flops=products, bytes_accessed=rows * width * 22, transcendentals=rows * LEN * pairs * 2
        ),
        name="attention",
    )(projected, projected, projected, attended_back, *tables)


def on_device(row, col, here, there):
    same = (lax.axis_index("rows") == row) & (lax.axis_index("cols") == col)
    pl.when(same)(here)
    pl.when(jnp.logical_not(same))(there)


def to_all(rows, cols, source_of, goal, send, take):
    row, col = lax.axis_index("rows"), lax.axis_index("cols")

    def one(place, carry):
        to_row, to_col = place // cols, lax.rem(place, cols)
        source = source_of(place)

        def here():
            pltpu.make_async_copy(source, goal, take).start()

        def there():
            pltpu.make_async_remote_copy(
                source, goal, send, take, device_id=(to_row, to_col), device_id_type=MESH
            ).start()

        on_device(to_row, to_col, here, there)
        return carry

    lax.fori_loop(0, rows * cols, one, 0)


def collect_kernel(
    widths, rows, cols, from_ref, vector_ref, to_ref, pieces_ref,
    send, take, cross_send, cross_take, piece_send, piece_take,
):
    row, col = lax.axis_index("rows"), lax.axis_index("cols")
    half_rows = rows // 2
    depth = from_ref.shape[0]
    half_depth = depth * half_rows
    start = 0
    for place, width in enumerate(widths):
        chip, plane = OWNERS[place]
        target = 2 * chip + row // half_rows
        source = from_ref.at[:, pl.ds(start, width)]
        goal = to_ref.at[pl.ds(row * depth, depth), pl.ds(col * width, width)]

        def here(source=source, goal=goal):
            pltpu.make_async_copy(source, goal, take).start()

        def there(source=source, goal=goal, target=target, plane=plane, place=place):
            pltpu.make_async_remote_copy(
                source, goal, send.at[place], take, device_id=(target, plane), device_id_type=MESH
            ).start()

        on_device(target, plane, here, there)
        start += width
    me = row * cols + col
    to_all(rows, cols, lambda place: vector_ref.at[place], pieces_ref.at[me], piece_send, piece_take)
    for place, width in enumerate(widths):
        chip, plane = OWNERS[place]
        core = lax.rem(row, 2)

        @pl.when((row // 2 == chip) & (col == plane))
        def _(width=width, core=core, plane=plane):
            own = to_ref.at[pl.ds(core * half_depth, half_depth), pl.ds(0, cols * width)]
            pltpu.make_async_copy(own, own, take).wait()
            swap = pltpu.make_async_remote_copy(
                own,
                own,
                cross_send,
                cross_take,
                device_id=(row + 1 - 2 * core, plane),
                device_id_type=MESH,
            )
            swap.start()
            other = to_ref.at[pl.ds((1 - core) * half_depth, half_depth), pl.ds(0, cols * width)]
            swap.wait_send()
            pltpu.make_async_copy(other, other, cross_take).wait()

    start = 0
    for place, width in enumerate(widths):
        chip, plane = OWNERS[place]
        source = from_ref.at[:, pl.ds(start, width)]

        def sent(source=source, place=place):
            pltpu.make_async_copy(source, source, send.at[place]).wait()

        on_device(2 * chip + row // half_rows, plane, lambda: None, sent)
        start += width
    pltpu.make_async_copy(pieces_ref, pieces_ref, piece_take).wait()
    others = vector_ref.at[pl.ds(0, rows * cols - 1)]
    pltpu.make_async_copy(others, others, piece_send).wait()


def collect(moments, vector, widths, rows, cols):
    depth = moments.shape[0]
    return pl.pallas_call(
        partial(collect_kernel, widths, rows, cols),
        in_specs=[pl.BlockSpec(memory_space=pl.ANY)] * 2,
        out_specs=[pl.BlockSpec(memory_space=pl.ANY)] * 2,
        out_shape=[
            jax.ShapeDtypeStruct((depth * rows, cols * max(widths)), BF16),
            jax.ShapeDtypeStruct(vector.shape, F32),
        ],
        scratch_shapes=[pltpu.SemaphoreType.DMA((6,))] + [pltpu.SemaphoreType.DMA] * 5,
        compiler_params=pltpu.CompilerParams(has_side_effects=True),
        name="collect",
    )(moments, vector)


def spread_kernel(
    widths, rows, cols, from_ref, piece_ref, to_ref, pieces_ref, send, take, piece_send, piece_take
):
    row, col = lax.axis_index("rows"), lax.axis_index("cols")
    half_rows = rows // 2
    depth = to_ref.shape[0]
    core = lax.rem(row, 2)
    start = 0
    for place, width in enumerate(widths):
        chip, plane = OWNERS[place]

        @pl.when((row // 2 == chip) & (col == plane))
        def _(width=width, start=start):
            def one(number, carry):
                near, to_col = number // cols, lax.rem(number, cols)
                to_row = core * half_rows + near
                source = from_ref.at[pl.ds(near * depth, depth), pl.ds(to_col * width, width)]
                goal = to_ref.at[:, pl.ds(start, width)]

                def here():
                    pltpu.make_async_copy(source, goal, take).start()

                def there():
                    pltpu.make_async_remote_copy(
                        source, goal, send, take, device_id=(to_row, to_col), device_id_type=MESH
                    ).start()

                on_device(to_row, to_col, here, there)
                return carry

            lax.fori_loop(0, half_rows * cols, one, 0)

        start += width
    goal = pieces_ref.at[row * cols + col]
    to_all(rows, cols, lambda place: piece_ref, goal, piece_send, piece_take)
    pltpu.make_async_copy(to_ref, to_ref, take).wait()
    for place, width in enumerate(widths):
        chip, plane = OWNERS[place]

        @pl.when((row // 2 == chip) & (col == plane))
        def _(width=width):
            def one(number, carry):
                near, to_col = number // cols, lax.rem(number, cols)
                source = from_ref.at[pl.ds(near * depth, depth), pl.ds(to_col * width, width)]

                def sent():
                    pltpu.make_async_copy(source, source, send).wait()

                on_device(core * half_rows + near, to_col, lambda: None, sent)
                return carry

            lax.fori_loop(0, half_rows * cols, one, 0)

    pltpu.make_async_copy(pieces_ref, pieces_ref, piece_take).wait()
    others = pieces_ref.at[pl.ds(0, rows * cols - 1)]
    pltpu.make_async_copy(others, others, piece_send).wait()


def spread(update, piece, widths, rows, cols):
    depth = D // rows
    return pl.pallas_call(
        partial(spread_kernel, widths, rows, cols),
        in_specs=[pl.BlockSpec(memory_space=pl.ANY)] * 2,
        out_specs=[pl.BlockSpec(memory_space=pl.ANY)] * 2,
        out_shape=[
            jax.ShapeDtypeStruct((depth, sum(widths)), BF16),
            jax.ShapeDtypeStruct((rows * cols,) + piece.shape, F32),
        ],
        scratch_shapes=[pltpu.SemaphoreType.DMA] * 4,
        compiler_params=pltpu.CompilerParams(has_side_effects=True),
        name="spread",
    )(update, piece)


def swap_kernel(part_ref, whole_ref, send, take):
    row, col = lax.axis_index("rows"), lax.axis_index("cols")
    depth = part_ref.shape[0]
    core = lax.rem(row, 2)
    mine = whole_ref.at[pl.ds(pl.multiple_of(core * depth, depth), depth), :]
    copy = pltpu.make_async_remote_copy(
        part_ref, mine, send, take, device_id=(row + 1 - 2 * core, col), device_id_type=MESH
    )
    copy.start()
    whole_ref[pl.ds(pl.multiple_of(core * depth, depth), depth), :] = part_ref[...]
    copy.wait()


def swap(part):
    depth, width = part.shape
    return pl.pallas_call(
        swap_kernel,
        in_specs=[pl.BlockSpec(memory_space=pltpu.VMEM)],
        out_specs=pl.BlockSpec(memory_space=pltpu.VMEM),
        out_shape=jax.ShapeDtypeStruct((2 * depth, width), part.dtype),
        scratch_shapes=[pltpu.SemaphoreType.DMA, pltpu.SemaphoreType.DMA],
        compiler_params=pltpu.CompilerParams(has_side_effects=True),
        name="swap",
    )(part)


def orthogonalize(moments, vector, widths, rows, cols):
    size = vector.shape[0]
    lines = -(-size // (rows * cols * 128))
    vector = jnp.pad(vector, (0, rows * cols * lines * 128 - size))
    row, col = lax.axis_index("rows"), lax.axis_index("cols")
    core = row % 2
    half = D // 2
    collected, pieces = collect(
        moments, vector.reshape(rows * cols, lines, 128), widths, rows, cols
    )
    own_width = jnp.int32(0)
    for (chip, plane), width in zip(OWNERS, widths):
        own_width = jnp.where((row // 2 == chip) & (col == plane), cols * width, own_width)
    kept = lax.broadcasted_iota(jnp.int32, collected.shape, 1) < own_width
    matrix = jnp.where(kept, collected, jnp.zeros_like(collected))
    part = times_transpose(lax.dynamic_slice_in_dim(matrix, core * half, half), matrix)
    whole = swap(part)
    place = lax.broadcasted_iota(jnp.int32, whole.shape, 0) == lax.broadcasted_iota(
        jnp.int32, whole.shape, 1
    )
    total = jnp.sum(jnp.where(place, whole, 0.0))
    shrink = 1.0 / (jnp.sqrt(total) + NORM_FLOOR)
    gram = (whole * shrink) * shrink
    part = (part * shrink) * shrink
    unit = (
        lax.broadcasted_iota(jnp.int32, part.shape, 0) + core * half
        == lax.broadcasted_iota(jnp.int32, part.shape, 1)
    ).astype(F32)
    product = None
    for step in range(ITERS):
        final = step == ITERS - 1
        if product is None:
            first = three_pass(part, gram)
            changed = COEF_FIRST * part + COEF_SECOND * first + COEF_THIRD * three_pass(first, gram)
            product = COEF_FIRST * unit + COEF_SECOND * part + COEF_THIRD * first
        elif final:
            first = three_pass(product, gram)
            product = (
                COEF_FIRST * product + COEF_SECOND * first + COEF_THIRD * three_pass(first, gram)
            )
        else:
            both = jnp.concatenate([part, product], axis=0)
            first = three_pass(both, gram)
            both = COEF_FIRST * both + COEF_SECOND * first + COEF_THIRD * three_pass(first, gram)
            changed, product = both[:half], both[half:]
        if not final:
            first = three_pass(changed, gram)
            part = (
                COEF_FIRST * changed + COEF_SECOND * first + COEF_THIRD * three_pass(first, gram)
            )
            gram = swap(part)
    high = product.astype(BF16)
    rest = (product - high.astype(F32)).astype(BF16)
    update = (low_product(high, matrix) + low_product(rest, matrix)) * shrink
    update, total = spread(update.astype(BF16), jnp.sum(pieces, 0), widths, rows, cols)
    return update, total.reshape(-1)[:size]


def split_sum(part_of, cols):
    col = lax.axis_index("cols")
    if cols == 2:
        sent = part_of(1 - col).astype(BF16)
        taken = lax.ppermute(sent, "cols", [(0, 1), (1, 0)])
        return part_of(col) + taken.astype(F32)
    parts = jnp.concatenate([part_of(place) for place in range(cols)], axis=1)
    return lax.psum_scatter(parts, "cols", scatter_dimension=1, tiled=True)


def whole_width(own, cols):
    if cols == 2:
        col, width = lax.axis_index("cols"), own.shape[1]
        taken = lax.ppermute(own, "cols", [(0, 1), (1, 0)])
        whole = jnp.zeros((own.shape[0], 2 * width), own.dtype)
        whole = lax.dynamic_update_slice(whole, own, (0, col * width))
        return lax.dynamic_update_slice(whole, taken, (0, (1 - col) * width))
    return lax.all_gather(own, "cols", axis=1, tiled=True)


def full_sum(value, cols):
    if cols == 2:
        return value + lax.ppermute(value, "cols", [(0, 1), (1, 0)])
    return lax.psum(value, "cols")


def shards(
    tokens,
    cotangent,
    first_gain,
    first_shift,
    second_gain,
    second_shift,
    query_weight,
    key_weight,
    value_weight,
    query_bias,
    value_bias,
    output_weight,
    up_weight,
    up_bias,
    down_weight,
    out_bias,
    first_gain_moment,
    first_shift_moment,
    second_gain_moment,
    second_shift_moment,
    query_moment,
    key_moment,
    value_moment,
    query_bias_moment,
    value_bias_moment,
    output_moment,
    up_moment,
    up_bias_moment,
    down_moment,
    out_bias_moment,
):
    rows = lax.axis_size("rows")
    cols = lax.axis_size("cols")
    col = lax.axis_index("cols")
    row_count, local_width = tokens.shape
    hidden_width = up_bias.shape[0]
    whole_tokens = whole_width(tokens, cols)
    forward_low = jnp.concatenate([up_weight.astype(BF16), down_weight.astype(BF16).T], axis=1)
    linear_low = jnp.concatenate(
        [
            query_weight.astype(BF16),
            key_weight.astype(BF16),
            value_weight.astype(BF16),
            output_weight.astype(BF16).T,
        ],
        axis=1,
    )
    forward_full = lax.all_gather(forward_low, "rows", axis=0, tiled=True)
    linear_full = lax.all_gather(linear_low, "rows", axis=0, tiled=True)
    whole_cotangent = whole_width(cotangent, cols)
    up_full = forward_full[:, :hidden_width]
    down_full = forward_full[:, hidden_width:]
    projection = linear_full[:, : 3 * local_width]
    output_full = linear_full[:, 3 * local_width :]
    tokens_f = whole_tokens.astype(F32)
    mean_value = jnp.mean(tokens_f, -1, keepdims=True)
    centered = tokens_f - mean_value
    inverse_scale = lax.rsqrt(jnp.mean(centered * centered, -1, keepdims=True) + EPSILON)
    normed = centered * inverse_scale
    first_input = (normed * first_gain + first_shift).astype(BF16)
    second_input = (normed * second_gain + second_shift).astype(BF16)
    up_linear = low_product(second_input, up_full) + up_bias
    activation, activation_back = jax.vjp(partial(jax.nn.gelu, approximate=False), up_linear)
    hidden = activation.astype(BF16)
    hidden_back = low_product(whole_cotangent, down_full)
    up_back = activation_back(hidden_back)[0].astype(BF16)

    def reduced(part):
        return lax.psum_scatter(part, "rows", scatter_dimension=0, tiled=True)

    down_part, up_part = inner_rows(whole_cotangent, hidden), inner_rows(second_input, up_back)
    down_part, up_part, first_input = lax.optimization_barrier((down_part, up_part, first_input))
    down_sums, up_sums = reduced(down_part), reduced(up_part)
    linear_bias = jnp.concatenate([query_bias, jnp.zeros_like(query_bias), value_bias])
    projected = low_product(first_input, projection) + linear_bias
    attended_back = low_product(whole_cotangent, output_full).astype(BF16)
    attended_low, query_back, key_back, value_back = attention(
        projected, attended_back, rotary_tables()
    )

    projected_back = jnp.concatenate([query_back, key_back, value_back], axis=1)
    other_part = jnp.concatenate(
        [inner_rows(first_input, projected_back), inner_rows(whole_cotangent, attended_low)], axis=1
    )
    other_part, attended_low, projected_back = lax.optimization_barrier(
        (other_part, attended_low, projected_back)
    )
    other_sums = reduced(other_part)

    def branch_part(place):
        output_part = lax.dynamic_slice_in_dim(output_full, place * local_width, local_width)
        down_part = lax.dynamic_slice_in_dim(down_full, place * local_width, local_width)
        return times_transpose(attended_low, output_part) + times_transpose(hidden, down_part)

    branch_share = split_sum(branch_part, cols)
    result = (tokens.astype(F32) + branch_share + out_bias).astype(BF16)
    first_back = times_transpose(projected_back, projection)
    second_back = times_transpose(up_back, up_full)
    norm_partials = jnp.stack(
        [
            jnp.sum(first_back * normed, 0),
            jnp.sum(first_back, 0),
            jnp.sum(second_back * normed, 0),
            jnp.sum(second_back, 0),
        ]
    )
    normed_part = first_back * first_gain + second_back * second_gain
    row_sums = full_sum(
        jnp.stack([jnp.sum(normed_part, 1), jnp.sum(normed_part * normed, 1)]), cols
    )
    normed_back = split_sum(
        lambda place: lax.dynamic_slice_in_dim(normed_part, place * local_width, local_width, 1),
        cols,
    )
    own_normed = (tokens.astype(F32) - mean_value) * inverse_scale
    back_mean = (row_sums[0] / D)[:, None]
    cross_mean = (row_sums[1] / D)[:, None]
    tokens_grad = (
        cotangent.astype(F32)
        + (normed_back - back_mean - own_normed * cross_mean) * inverse_scale
    )
    query_weight_grad = other_sums[:, :local_width]
    key_weight_grad = other_sums[:, local_width : 2 * local_width]
    value_weight_grad = other_sums[:, 2 * local_width : 3 * local_width]
    up_weight_grad = up_sums
    output_weight_grad = other_sums[:, 3 * local_width :].T
    down_weight_grad = down_sums.T
    bias_partials = jnp.concatenate(
        [
            jnp.sum(query_back, 0, dtype=F32),
            jnp.sum(value_back, 0, dtype=F32),
            jnp.sum(up_back, 0, dtype=F32),
            jnp.sum(cotangent, 0, dtype=F32),
        ]
    )
    slots = jnp.where(
        lax.broadcasted_iota(jnp.int32, (cols, bias_partials.shape[0]), 0) == col,
        bias_partials[None],
        0.0,
    )
    query_moment_new = MOMENTUM * query_moment + query_weight_grad
    key_moment_new = MOMENTUM * key_moment + key_weight_grad
    value_moment_new = MOMENTUM * value_moment + value_weight_grad
    up_moment_new = MOMENTUM * up_moment + up_weight_grad
    output_moment_new = MOMENTUM * output_moment + output_weight_grad
    down_moment_new = MOMENTUM * down_moment + down_weight_grad
    oriented = (
        query_moment_new,
        key_moment_new,
        value_moment_new,
        up_moment_new,
        output_moment_new.T,
        down_moment_new.T,
    )
    widths = tuple(moment.shape[1] for moment in oriented)
    bounds = [sum(widths[:position]) for position in range(7)]
    packed, totals = orthogonalize(
        jnp.concatenate([moment.astype(BF16) for moment in oriented], axis=1),
        jnp.concatenate([norm_partials.reshape(-1), slots.reshape(-1)]),
        widths,
        rows,
        cols,
    )
    packed = packed.astype(F32)
    norm_totals = totals[: 4 * D].reshape(4, D)
    bias_totals = lax.dynamic_index_in_dim(
        totals[4 * D :].reshape(slots.shape), col, 0, keepdims=False
    )
    query_bias_grad = bias_totals[:local_width]
    value_bias_grad = bias_totals[local_width : 2 * local_width]
    up_bias_grad = bias_totals[2 * local_width : 2 * local_width + hidden_width]
    out_bias_grad = bias_totals[2 * local_width + hidden_width :]
    orthogonal = [packed[:, bounds[position] : bounds[position + 1]] for position in range(6)]
    up_scale = math.sqrt(max(1.0, FF / D))
    query_weight_new = query_weight - MATRIX_RATE * orthogonal[0]
    key_weight_new = key_weight - MATRIX_RATE * orthogonal[1]
    value_weight_new = value_weight - MATRIX_RATE * orthogonal[2]
    up_weight_new = up_weight - MATRIX_RATE * (up_scale * orthogonal[3])
    output_weight_new = output_weight - MATRIX_RATE * orthogonal[4].T
    down_weight_new = down_weight - MATRIX_RATE * orthogonal[5].T
    vector_step = VECTOR_RATE / math.sqrt(row_count * rows)
    first_gain_grad = norm_totals[0]
    first_shift_grad = norm_totals[1]
    second_gain_grad = norm_totals[2]
    second_shift_grad = norm_totals[3]
    first_gain_moment_new = MOMENTUM * first_gain_moment + first_gain_grad
    first_shift_moment_new = MOMENTUM * first_shift_moment + first_shift_grad
    second_gain_moment_new = MOMENTUM * second_gain_moment + second_gain_grad
    second_shift_moment_new = MOMENTUM * second_shift_moment + second_shift_grad
    query_bias_moment_new = MOMENTUM * query_bias_moment + query_bias_grad
    value_bias_moment_new = MOMENTUM * value_bias_moment + value_bias_grad
    up_bias_moment_new = MOMENTUM * up_bias_moment + up_bias_grad
    out_bias_moment_new = MOMENTUM * out_bias_moment + out_bias_grad
    first_gain_new = first_gain - vector_step * first_gain_moment_new
    first_shift_new = first_shift - vector_step * first_shift_moment_new
    second_gain_new = second_gain - vector_step * second_gain_moment_new
    second_shift_new = second_shift - vector_step * second_shift_moment_new
    query_bias_new = query_bias - vector_step * query_bias_moment_new
    value_bias_new = value_bias - vector_step * value_bias_moment_new
    up_bias_new = up_bias - vector_step * up_bias_moment_new
    out_bias_new = out_bias - vector_step * out_bias_moment_new
    return (
        result,
        tokens_grad,
        first_gain_grad,
        first_shift_grad,
        second_gain_grad,
        second_shift_grad,
        query_weight_grad,
        key_weight_grad,
        value_weight_grad,
        query_bias_grad,
        value_bias_grad,
        output_weight_grad,
        up_weight_grad,
        up_bias_grad,
        down_weight_grad,
        out_bias_grad,
        first_gain_moment_new,
        first_shift_moment_new,
        second_gain_moment_new,
        second_shift_moment_new,
        query_moment_new,
        key_moment_new,
        value_moment_new,
        query_bias_moment_new,
        value_bias_moment_new,
        output_moment_new,
        up_moment_new,
        up_bias_moment_new,
        down_moment_new,
        out_bias_moment_new,
        first_gain_new,
        first_shift_new,
        second_gain_new,
        second_shift_new,
        query_weight_new,
        key_weight_new,
        value_weight_new,
        query_bias_new,
        value_bias_new,
        output_weight_new,
        up_weight_new,
        up_bias_new,
        down_weight_new,
        out_bias_new,
    )


def solution(mesh):
    in_specs = (
        P("rows", "cols"),
        P("rows", "cols"),
        P(),
        P(),
        P(),
        P(),
        P("rows", "cols"),
        P("rows", "cols"),
        P("rows", "cols"),
        P("cols"),
        P("cols"),
        P("cols", "rows"),
        P("rows", "cols"),
        P("cols"),
        P("cols", "rows"),
        P("cols"),
        P(),
        P(),
        P(),
        P(),
        P("rows", "cols"),
        P("rows", "cols"),
        P("rows", "cols"),
        P("cols"),
        P("cols"),
        P("cols", "rows"),
        P("rows", "cols"),
        P("cols"),
        P("cols", "rows"),
        P("cols"),
    )
    out_specs = (
        P("rows", "cols"),
        P("rows", "cols"),
        P(),
        P(),
        P(),
        P(),
        P("rows", "cols"),
        P("rows", "cols"),
        P("rows", "cols"),
        P("cols"),
        P("cols"),
        P("cols", "rows"),
        P("rows", "cols"),
        P("cols"),
        P("cols", "rows"),
        P("cols"),
        P(),
        P(),
        P(),
        P(),
        P("rows", "cols"),
        P("rows", "cols"),
        P("rows", "cols"),
        P("cols"),
        P("cols"),
        P("cols", "rows"),
        P("rows", "cols"),
        P("cols"),
        P("cols", "rows"),
        P("cols"),
        P(),
        P(),
        P(),
        P(),
        P("rows", "cols"),
        P("rows", "cols"),
        P("rows", "cols"),
        P("cols"),
        P("cols"),
        P("cols", "rows"),
        P("rows", "cols"),
        P("cols"),
        P("cols", "rows"),
        P("cols"),
    )
    return jax.shard_map(shards, mesh=mesh, in_specs=in_specs, out_specs=out_specs, check_vma=False)
```

time: 3340 us -> 1030 us (0.31)
  waiting for transfers between devices: 2040 us -> 336 us
  matrix products: 771 us -> 331 us
  Pallas kernels: 0 us -> 251 us
  local copies, waits for them, and re-layouts: 260 us -> 23 us
  blocking collectives: 87.9 us -> 0 us
  other arithmetic: 127 us -> 57.3 us
    all_gather x19 -> x2, waiting for transfers between devices: 1430 us -> 19.2 us  [the longest x1 19.2 us: shards(): forward_full = lax.all_gather(forward_low, 'rows', axis=0, tiled=True)]
    dot_general x122 -> x24, matrix products: 671 us -> 220 us  [the longest x6 111 us: low_product(): return jnp.dot(left, right, preferred_element_type=F32)]
    pallas_call x0 -> x8, Pallas kernels: none -> 251 us  [the longest x5 79.6 us: swap(): pl.pallas_call(swap_kernel, in_specs=[pl.BlockSpec(memory_space=pltpu.VME...]
    psum x5 -> x0, waiting for transfers between devices: 233 us -> none  [shards(): lax.psum(jnp.stack([outer_high(gathered[:, bounds[position]:bounds[positi...]
    reduce_scatter x3, waiting for transfers between devices: 383 us -> 177 us  [reduced(): return lax.psum_scatter(part, 'rows', scatter_dimension=0, tiled=True)]
    dynamic_update_slice x8 -> x4, local copies, waits for them, and re-layouts: 160 us -> 6.94 us  [the longest x2 5.03 us: whole_width(): return lax.dynamic_update_slice(whole, taken, (0, (1 - col) * width))]
    ppermute x0 -> x5, waiting for transfers between devices: none -> 140 us  [the longest x2 77.6 us: whole_width(): taken = lax.ppermute(own, 'cols', [(0, 1), (1, 0)])]
    psum x2 -> x0, blocking collectives: 87.9 us -> none  [the longest x1 47.1 us: shards(): lax.psum((jnp.sum(query_back, 0, dtype=jnp.float32), jnp.sum(value_back,...]
  transfers between devices with their start and end apart: 27 -> 10, of which waited for: 24 -> 7; matrix products, arithmetic and copies ran while one was open for 19% -> 10% of each run, Pallas kernels for 0% -> 0%
where the time goes in v1:
time: 1030 us; the launch traced here: 1020 us
  waiting for transfers between devices  336 us (33%)
  matrix products  331 us (32%)
  Pallas kernels  251 us (24%)
  other arithmetic  57.3 us (6%)
  local copies, waits for them, and re-layouts  23 us (2%)
  between operations  15.9 us (2%)
    reduce_scatter x3, waiting for transfers between devices, reduced(): return lax.psum_scatter(part, 'rows', scatter_dimension=0, tiled=True)  177 us
    dot_general x6, matrix products, low_product(): return jnp.dot(left, right, preferred_element_type=F32)  111 us
    dot_general x18, matrix products, three_pass(): return jnp.dot(left, right, precision=lax.Precision.HIGH)  109 us
    pallas_call x5, Pallas kernels, swap(): pl.pallas_call(swap_kernel, in_specs=[pl.BlockSpec(memory_space=pltpu.VME...  79.6 us
    ppermute x2, waiting for transfers between devices, whole_width(): taken = lax.ppermute(own, 'cols', [(0, 1), (1, 0)])  77.6 us
    pallas_call x1, Pallas kernels, attention(): pl.pallas_call(attention_kernel, grid=(rows // LEN, pairs), in_specs=[pla...  70.9 us
    dot_general x7, matrix products, times_transpose(): lax.dot_general(left, right, (((1,), (1,)), ((), ())), preferred_element_...  67.3 us
    pallas_call x1, Pallas kernels, spread(): pl.pallas_call(partial(spread_kernel, widths, rows, cols), in_specs=[pl.B...  55.1 us
  transfers between devices with their start and end apart: 10, of which 7 were waited for; matrix products, arithmetic and copies ran while one was open for 10% of the time, Pallas kernels for 0%

profile of v1, /device:TPU:15, one launch (start us, length us, event | category | flops | bytes accessed | tf_op | source)
XLA Modules:
  0.0 1018.8 jit_solution(17105765806835025085)
XLA Ops:
  25.2 36.7 %collective-permute-done.1 = bf16[2048,512]{1,0:T(8,128)(2,1)} collective-permute-done((bf16[2048,512]{1,0:T(8,128)(2,1)}, bf16[2048,512]{1,0:T(8,128)(2,1)}, u32[]{:S(2)}, u32[]{:S(2)}) %collective-permute-start.1) | collective-permute-done | bytes 2097184 | tf_op jit(solution)/shard_map/ppermute | solution.py:431
  65.9 40.9 %collective-permute-done = bf16[2048,512]{1,0:T(8,128)(2,1)} collective-permute-done((bf16[2048,512]{1,0:T(8,128)(2,1)S(1)}, bf16[2048,512]{1,0:T(8,128)(2,1)}, u32[]{:S(2)}, u32[]{:S(2)}) %collective-permute-start) | collective-permute-done | bytes 2097184 | tf_op jit(solution)/shard_map/ppermute | solution.py:431
  119.2 19.2 %all-gather.3.cloned.1.call-done = bf16[1024,4096]{1,0:T(8,128)(2,1)} async-done(((bf16[64,4096]{1,0:T(8,128)(2,1)}), bf16[1024,4096]{1,0:T(8,128)(2,1)}) %all-gather.3.cloned.1.call-update) | async-done | bytes 8388624 | tf_op jit(solution)/shard_map/all_gather | solution.py:492
  138.3 51.2 %multiply_convert_fusion = (bf16[2048,2048]{1,0:T(8,128)(2,1)}, f32[2048,2048]{1,0:T(8,128)}, f32[2048,2048]{1,0:T(8,128)}) fusion(f32[2048]{0:T(1024)S(1)} %copy-done.45, bf16[1024,4096]{1,0:T(8,128)(2,1)} %all-gather.3.cloned.1.call-done, bf16[2048,1024]{1,0:T(8,128)(2,1)} %copy-done.7, f32[1024]{0:T(1024)S(1)} %copy-done.56, f32[1024]{0:T(1024)S(1)} %copy-done.58, ...), kind=kOutput, calls=%fused_computation.4 | convolution fusion | flops 8879341568 | bytes 50364416 | tf_op jit(solution)/shard_map/dot_general | solution.py:37
  189.6 27.6 %convert_reduce_fusion = (f32[2048]{0:T(1024)S(1)}, bf16[2048,2048]{1,0:T(8,128)(2,1)}) fusion(f32[2048,2048]{1,0:T(8,128)} %get-tuple-element.120, bf16[2048,1024]{1,0:T(8,128)(2,1)} %constant_dynamic-update-slice_fusion.5, bf16[1024,4096]{1,0:T(8,128)(2,1)} %all-gather.3.cloned.1.call-done, f32[2048,2048]{1,0:T(8,128)} %get-tuple-element.143, ...), kind=kOutput, calls=%fused_computation.2 | convolution fusion | flops 8661235712 | bytes 50348032 | tf_op jit(solution)/shard_map/dot_general | solution.py:37
  217.2 15.7 %fusion.92 = f32[1024,2048]{1,0:T(8,128)} fusion(bf16[2048,2048]{1,0:T(8,128)(2,1)} %get-tuple-element.145, bf16[2048,1024]{1,0:T(8,128)(2,1)} %copy-done.7, f32[1024]{0:T(1024)S(1)} %copy-done.56, f32[1024]{0:T(1024)S(1)} %copy-done.58, f32[2048]{0:T(1024)S(1)} %add_rsqrt_fusion, f32[2048]{0:T(1024)S(1)} %broadcast_multiply_fusion), kind=kOutput, calls=%fused_computation.211 | convolution fusion | flops 8602517504 | bytes 20996096 | tf_op jit(solution)/shard_map/dot_general | solution.py:45
  232.9 14.6 %fusion.98 = f32[1024,2048]{1,0:T(8,128)} fusion(bf16[2048,1024]{1,0:T(8,128)(2,1)} %constant_dynamic-update-slice_fusion.5, bf16[2048,2048]{1,0:T(8,128)(2,1)} %get-tuple-element.119), kind=kOutput, calls=%fused_computation.214 | convolution fusion | flops 8589934592 | bytes 20971520 | tf_op jit(solution)/shard_map/dot_general | solution.py:45
  247.6 12.6 %convolution_add_fusion.query_ref.key_ref.value_ref = f32[2048,1536]{1,0:T(8,128)} fusion(bf16[2048,1024]{1,0:T(8,128)(2,1)} %fusion.16, f32[1536]{0:T(1024)S(1)} %copy-done.55, bf16[1024,2048]{1,0:T(8,128)(2,1)} %all-gather.5.cloned.1.call-done), kind=kOutput, calls=%fused_computation.27 | convolution fusion | flops 6445596672 | bytes 19929088 | tf_op jit(solution)/shard_map/dot_general | solution.py:37
  260.2 70.9 %attention.1 = (bf16[2048,512]{1,0:T(8,128)(2,1)S(1)}, bf16[2048,512]{1,0:T(8,128)(2,1)S(1)}, bf16[2048,512]{1,0:T(8,128)(2,1)S(1)}, bf16[2048,512]{1,0:T(8,128)(2,1)S(1)}) custom-call(f32[2048,1536]{1,0:T(8,128)} %convolution_add_fusion.query_ref.key_ref.value_ref, f32[2048,1536]{1,0:T(8,128)} %convolution_add_fusion.query_ref.key_ref.value_ref, ...), custom_call_target="tpu_custom_call" | custom-call | flops 12884901888 | bytes 23068672 | tf_op jit(solution)/shard_map/attention/pallas_call | solution.py:131
  334.8 9.2 fusion.99
  358.1 15.0 %fusion.29 = f32[2048,1024]{1,0:T(8,128)} fusion(bf16[2048,2048]{1,0:T(8,128)(2,1)} %get-tuple-element.145, bf16[1024,4096]{1,0:T(8,128)(2,1)} %all-gather.3.cloned.1.call-done), kind=kOutput, calls=%fused_computation.65 | convolution fusion | flops 8589934592 | bytes 20971520 | tf_op jit(solution)/shard_map/dot_general | solution.py:41
  373.2 14.9 %fusion.95 = (f32[2048]{0:T(1024)S(1)}, f32[2048]{0:T(1024)S(1)}, f32[1024]{0:T(1024)S(1)}, f32[1024]{0:T(1024)S(1)}, f32[1024]{0:T(1024)S(1)}, /*index=5*/f32[1024]{0:T(1024)S(1)}, f32[2048,1024]{1,0:T(8,128)S(1)}) fusion(f32[2048]{0:T(1024)S(1)} %add_rsqrt_fusion, f32[2048]{0:T(1024)S(1)} %broadcast_multiply_fusion, ...), kind=kOutput, calls=%fused_computation.212 | convolution fusion | flops 6473900032 | bytes 30466048 | tf_op jit(solution)/shard_map/dot_general | solution.py:41
  403.1 9.8 fusion.49
  413.6 22.2 %collective-permute-done.4 = f32[2,2048]{1,0:T(2,128)S(1)} collective-permute-done((f32[2,2048]{1,0:T(2,128)S(1)}, f32[2,2048]{1,0:T(2,128)S(1)}, u32[]{:S(2)}, u32[]{:S(2)}) %collective-permute-start.4) | collective-permute-done | bytes 16416 | tf_op jit(solution)/shard_map/ppermute | solution.py:440
  440.5 40.3 %collective-permute-done.2 = bf16[2048,512]{1,0:T(8,128)(2,1)} collective-permute-done((bf16[2048,512]{1,0:T(8,128)(2,1)}, bf16[2048,512]{1,0:T(8,128)(2,1)}, u32[]{:S(2)}, u32[]{:S(2)}) %collective-permute-start.2) | collective-permute-done | bytes 2097184 | tf_op jit(solution)/shard_map/ppermute | solution.py:422
  480.8 7.3 fusion.22
  493.1 72.8 %reduce-scatter.6.cloned.1.call-done = f32[64,2048]{1,0:T(8,128)} async-done(((f32[1024,2048]{1,0:T(8,128)}), f32[64,2048]{1,0:T(8,128)}) %reduce-scatter.6.cloned.1.call-update) | async-done | bytes 524304 | tf_op jit(solution)/shard_map/reduce_scatter | solution.py:513
  569.6 103.8 %reduce-scatter.8.cloned.1.call-done = f32[64,2048]{1,0:T(8,128)} async-done(((f32[1024,2048]{1,0:T(8,128)}), f32[64,2048]{1,0:T(8,128)}) %reduce-scatter.8.cloned.1.call-update) | async-done | bytes 524304 | tf_op jit(solution)/shard_map/reduce_scatter | solution.py:513
  676.3 45.0 %collect.1 = (bf16[1024,4096]{1,0:T(8,128)(2,1)}, f32[32,3,128]{2,1,0:T(4,128)}) custom-call(bf16[64,6144]{1,0:T(8,128)(2,1)} %copy-done.28, f32[32,3,128]{2,1,0:T(4,128)} %reshape.181.vector_ref), custom_call_target="tpu_custom_call" | custom-call | tf_op jit(solution)/shard_map/collect/pallas_call | solution.py:246
  721.3 7.2 broadcast_select_fusion
  728.5 10.5 %fusion.27.part_ref = f32[512,1024]{1,0:T(8,128)} fusion(bf16[1024,4096]{1,0:T(8,128)(2,1)} %broadcast_select_fusion, s32[]{:T(128)S(6)} %select_n.126), kind=kOutput, calls=%fused_computation.59 | convolution fusion | flops 4294967296 | bytes 14680068 | tf_op jit(solution)/shard_map/dot_general | solution.py:41
  739.0 27.1 %swap.5 = f32[1024,1024]{1,0:T(8,128)} custom-call(f32[512,1024]{1,0:T(8,128)} %fusion.27.part_ref), custom_call_target="tpu_custom_call" | custom-call | tf_op jit(solution)/shard_map/swap/pallas_call | solution.py:349
  769.8 7.4 multiply_add_fusion.8
  790.0 13.2 %swap.6 = f32[1024,1024]{1,0:T(8,128)} custom-call(f32[512,1024]{1,0:T(8,128)} %multiply_add_fusion.9.part_ref), custom_call_target="tpu_custom_call" | custom-call | tf_op jit(solution)/shard_map/swap/pallas_call | solution.py:349
  803.2 10.0 fusion.35
  831.1 13.2 %swap.7 = f32[1024,1024]{1,0:T(8,128)} custom-call(f32[512,1024]{1,0:T(8,128)} %multiply_add_fusion.7.part_ref), custom_call_target="tpu_custom_call" | custom-call | tf_op jit(solution)/shard_map/swap/pallas_call | solution.py:349
  844.3 10.0 fusion.34
  871.9 13.2 %swap.8 = f32[1024,1024]{1,0:T(8,128)} custom-call(f32[512,1024]{1,0:T(8,128)} %multiply_add_fusion.6.part_ref), custom_call_target="tpu_custom_call" | custom-call | tf_op jit(solution)/shard_map/swap/pallas_call | solution.py:349
  885.1 10.0 fusion.33
  895.1 7.2 multiply_add_fusion.1
  911.3 13.1 %swap.9 = f32[1024,1024]{1,0:T(8,128)} custom-call(f32[512,1024]{1,0:T(8,128)} %multiply_add_fusion.5.part_ref), custom_call_target="tpu_custom_call" | custom-call | tf_op jit(solution)/shard_map/swap/pallas_call | solution.py:349
  948.8 55.1 %spread.1 = (bf16[64,6144]{1,0:T(8,128)(2,1)}, f32[32,3,128]{2,1,0:T(4,128)}) custom-call(bf16[512,4096]{1,0:T(8,128)(2,1)} %multiply_convert_fusion.1.from_ref, f32[3,128]{1,0:T(4,128)} %reduce_sum.139.piece_ref), custom_call_target="tpu_custom_call" | custom-call | tf_op jit(solution)/shard_map/spread/pallas_call | solution.py:320
  (254 shorter events, 175.9 us)
Async XLA Ops:
  7.3 105.7 %all-gather.5.cloned.1.call-start = ((), (), s32[]{:S(2)}) async-start(), calls=%async_computation.4 | async-start | bytes 4456448 | tf_op jit(solution)/shard_map/all_gather | solution.py:493
  11.9 126.5 %all-gather.3.cloned.1.call-start = ((), (), s32[]{:S(2)}) async-start(), calls=%async_computation.3 | async-start | bytes 8912896 | tf_op jit(solution)/shard_map/all_gather | solution.py:492
  14.9 473.2 %reduce-scatter.4.cloned.1.call-start = ((), (), s32[]{:S(2)}) async-start(), calls=%async_computation.5 | async-start | bytes 8912896 | tf_op jit(solution)/shard_map/reduce_scatter | solution.py:513
  15.0 46.9 %collective-permute-start.1 = (bf16[2048,512]{1,0:T(8,128)(2,1)}, bf16[2048,512]{1,0:T(8,128)(2,1)}, u32[]{:S(2)}, u32[]{:S(2)}) collective-permute-start(bf16[2048,512]{1,0:T(8,128)(2,1)} %param.30), channel_id=1, source_target_pairs={{0,1},{1,0},{2,3},{3,2},{4,5},{5,4},{6,7},{7,6},{8,9},{9,8},{10,11... | collective-permute-start | bytes 6291464 | tf_op jit(solution)/shard_map/ppermute | solution.py:431
  15.3 91.5 %collective-permute-start = (bf16[2048,512]{1,0:T(8,128)(2,1)S(1)}, bf16[2048,512]{1,0:T(8,128)(2,1)}, u32[]{:S(2)}, u32[]{:S(2)}) collective-permute-start(bf16[2048,512]{1,0:T(8,128)(2,1)S(1)} %copy-done.17), channel_id=1, source_target_pairs={{0,1},{1,0},{2,3},{3,2},{4,5},{5,4},{6,7},{7,6},{8,9},{9,8},{10,11... | collective-permute-start | bytes 6291464 | tf_op jit(solution)/shard_map/ppermute | solution.py:431
  63.8 46.1 %copy-start.7 = (bf16[2048,1024]{1,0:T(8,128)(2,1)}, bf16[2048,1024]{1,0:T(8,128)(2,1)S(1)}, u32[]{:S(2)}) copy-start(bf16[2048,1024]{1,0:T(8,128)(2,1)S(1)} %constant_dynamic-update-slice_fusion.3) | copy-start | bytes 12582916
  64.4 45.5 %copy-start.41 = (f32[1024]{0:T(1024)S(1)}, f32[1024]{0:T(1024)}, u32[]{:S(2)}) copy-start(f32[1024]{0:T(1024)} %param.33) | copy-start | bytes 12292
  64.5 45.5 %copy-start.43 = (f32[1024]{0:T(1024)S(1)}, f32[1024]{0:T(1024)}, u32[]{:S(2)}) copy-start(f32[1024]{0:T(1024)} %param.32) | copy-start | bytes 12292
  113.0 25.4 %copy-start.45 = (f32[2048]{0:T(1024)S(1)}, f32[2048]{0:T(1024)}, u32[]{:S(2)}) copy-start(f32[2048]{0:T(1024)} %param.43) | copy-start | bytes 24580
  113.0 25.4 %copy-start.56 = (f32[1024]{0:T(1024)S(1)}, f32[1024]{0:T(1024)}, u32[]{:S(2)}) copy-start(f32[1024]{0:T(1024)} %param.35) | copy-start | bytes 12292
  113.0 25.4 %copy-start.58 = (f32[1024]{0:T(1024)S(1)}, f32[1024]{0:T(1024)}, u32[]{:S(2)}) copy-start(f32[1024]{0:T(1024)} %param.34) | copy-start | bytes 12292
  355.5 210.4 %reduce-scatter.6.cloned.1.call-start = ((), (), s32[]{:S(2)}) async-start(), calls=%async_computation.6 | async-start | bytes 8912896 | tf_op jit(solution)/shard_map/reduce_scatter | solution.py:513
  356.1 317.4 %reduce-scatter.8.cloned.1.call-start = ((), (), s32[]{:S(2)}) async-start(), calls=%async_computation.7 | async-start | bytes 8912896 | tf_op jit(solution)/shard_map/reduce_scatter | solution.py:513
  358.1 15.1 %copy-start.8 = (bf16[2048,1024]{1,0:T(8,128)(2,1)S(1)}, bf16[2048,1024]{1,0:T(8,128)(2,1)}, u32[]{:S(2)}) copy-start(bf16[2048,1024]{1,0:T(8,128)(2,1)} %copy-done.7) | copy-start | bytes 12582916
  358.1 15.0 %copy-start.44 = (f32[1024]{0:T(1024)S(1)}, f32[1024]{0:T(1024)}, u32[]{:S(2)}) copy-start(f32[1024]{0:T(1024)} %param.32) | copy-start | bytes 12292
  388.4 47.4 %collective-permute-start.3 = (bf16[2048,512]{1,0:T(8,128)(2,1)S(1)}, bf16[2048,512]{1,0:T(8,128)(2,1)S(1)}, u32[]{:S(2)}, u32[]{:S(2)}) collective-permute-start(bf16[2048,512]{1,0:T(8,128)(2,1)S(1)} %dynamic-slice_convert_fusion), channel_id=1, source_target_pairs={{0,1},{1,0},{2,3},{3,2},{4,5},{5,4},{6,7},{7,6},{8,9},{9,8},{10,11... | collective-permute-start | bytes 6291464 | tf_op jit(solution)/shard_map/ppermute | solution.py:422
  388.8 47.0 %collective-permute-start.4 = (f32[2,2048]{1,0:T(2,128)S(1)}, f32[2,2048]{1,0:T(2,128)S(1)}, u32[]{:S(2)}, u32[]{:S(2)}) collective-permute-start(f32[2,2048]{1,0:T(2,128)S(1)} %pad_maximum_fusion.9), channel_id=1, source_target_pairs={{0,1},{1,0},{2,3},{3,2},{4,5},{5,4},{6,7},{7,6},{8,9},{9,8},{10,11... | collective-permute-start | bytes 49160 | tf_op jit(solution)/shard_map/ppermute | solution.py:440
  403.0 32.8 %copy-start.18 = (bf16[2048,512]{1,0:T(8,128)(2,1)S(1)}, bf16[2048,512]{1,0:T(8,128)(2,1)}, u32[]{:S(2)}) copy-start(bf16[2048,512]{1,0:T(8,128)(2,1)} %param.31) | copy-start | bytes 6291460
  403.0 32.8 %copy-start.20 = (bf16[2048,512]{1,0:T(8,128)(2,1)S(1)}, bf16[2048,512]{1,0:T(8,128)(2,1)}, u32[]{:S(2)}) copy-start(bf16[2048,512]{1,0:T(8,128)(2,1)} %param.30) | copy-start | bytes 6291460
  412.9 67.9 %collective-permute-start.2 = (bf16[2048,512]{1,0:T(8,128)(2,1)}, bf16[2048,512]{1,0:T(8,128)(2,1)}, u32[]{:S(2)}, u32[]{:S(2)}) collective-permute-start(bf16[2048,512]{1,0:T(8,128)(2,1)} %add_convert_fusion.1), channel_id=1, source_target_pairs={{0,1},{1,0},{2,3},{3,2},{4,5},{5,4},{6,7},{7,6},{8,9},{9,8},{10,11... | collective-permute-start | bytes 6291464 | tf_op jit(solution)/shard_map/ppermute | solution.py:422
  435.8 45.0 %copy-start.63 = (f32[512]{0:T(512)S(1)}, f32[512]{0:T(512)}, u32[]{:S(2)}) copy-start(f32[512]{0:T(512)} %param.45) | copy-start | bytes 6148
  440.5 47.6 %copy-start.35 = (f32[64,512]{1,0:T(8,128)S(1)}, f32[64,512]{1,0:T(8,128)}, u32[]{:S(2)}) copy-start(f32[64,512]{1,0:T(8,128)} %param.50) | copy-start | bytes 393220
  440.5 49.3 %copy-start.36 = (f32[64,512]{1,0:T(8,128)S(1)}, f32[64,512]{1,0:T(8,128)}, u32[]{:S(2)}) copy-start(f32[64,512]{1,0:T(8,128)} %param.51) | copy-start | bytes 393220
  440.5 50.9 %copy-start.37 = (f32[64,512]{1,0:T(8,128)S(1)}, f32[64,512]{1,0:T(8,128)}, u32[]{:S(2)}) copy-start(f32[64,512]{1,0:T(8,128)} %param.52) | copy-start | bytes 393220
  488.1 185.3 %copy-start.30 = (f32[2048,64]{0,1:T(8,128)S(1)}, f32[2048,64]{0,1:T(8,128)}, u32[]{:S(2)}) copy-start(f32[2048,64]{0,1:T(8,128)} %param.58) | copy-start | bytes 1572868
  739.0 30.8 %copy-start.21 = (f32[512,1024]{1,0:T(8,128)S(1)}, f32[512,1024]{1,0:T(8,128)}, u32[]{:S(2)}) copy-start(f32[512,1024]{1,0:T(8,128)} %fusion.27.part_ref) | copy-start | bytes 6291460
  739.0 30.8 %copy-start.67 = (s32[512]{0:T(512)S(1)}, s32[512]{0:T(512)}, u32[]{:S(2)}) copy-start(s32[512]{0:T(512)} %iota_add_fusion) | copy-start | bytes 6148
  948.1 57.3 %copy-start.24 = (f32[2048,64]{0,1:T(8,128)S(1)}, f32[2048,64]{0,1:T(8,128)}, u32[]{:S(2)}) copy-start(f32[2048,64]{0,1:T(8,128)} %param.44) | copy-start | bytes 1572868
  948.1 58.2 %copy-start.25 = (f32[64,2048]{1,0:T(8,128)S(1)}, f32[64,2048]{1,0:T(8,128)}, u32[]{:S(2)}) copy-start(f32[64,2048]{1,0:T(8,128)} %param.42) | copy-start | bytes 1572868
  948.8 58.4 %copy-start.31 = (f32[64,512]{1,0:T(8,128)S(1)}, f32[64,512]{1,0:T(8,128)}, u32[]{:S(2)}) copy-start(f32[64,512]{1,0:T(8,128)} %param.38) | copy-start | bytes 393220
  948.8 58.4 %copy-start.32 = (f32[64,512]{1,0:T(8,128)S(1)}, f32[64,512]{1,0:T(8,128)}, u32[]{:S(2)}) copy-start(f32[64,512]{1,0:T(8,128)} %param.37) | copy-start | bytes 393220
  948.8 58.4 %copy-start.33 = (f32[64,512]{1,0:T(8,128)S(1)}, f32[64,512]{1,0:T(8,128)}, u32[]{:S(2)}) copy-start(f32[64,512]{1,0:T(8,128)} %param.36) | copy-start | bytes 393220
  (49 other events, 353.0 us)
Sparse Core Ops, SparseCore 0:
  12.0 51.0 all-gather.4
  65.8 72.5 all-gather.2
  355.6 102.5 reduce-scatter.3
  462.7 103.0 reduce-scatter.5
  570.3 103.0 reduce-scatter.7

commit v2 on v1

--- a/solution.py
+++ b/solution.py
@@ -43,10 +43,6 @@
 
 def inner_rows(left, right):
     return lax.dot_general(left, right, (((0,), (0,)), ((), ())), preferred_element_type=F32)
-
-
-def three_pass(left, right):
-    return jnp.dot(left, right, precision=lax.Precision.HIGH)
 
 
 def rotary_tables():
@@ -151,6 +147,56 @@
     )(projected, projected, projected, attended_back, *tables)
 
 
+def feed_forward_kernel(
+    input_ref, cotangent_ref, up_ref, down_ref, bias_ref, hidden_ref, back_ref, sum_ref
+):
+    @pl.when(pl.program_id(1) == 0)
+    def _():
+        sum_ref[...] = jnp.zeros_like(sum_ref)
+
+    up, down, bias = up_ref[...], down_ref[...], bias_ref[...]
+    total = jnp.zeros_like(bias)
+    size = 128
+    for number in range(input_ref.shape[0] // size):
+        place = slice(number * size, (number + 1) * size)
+        linear = low_product(input_ref[place, :], up) + bias
+        back = low_product(cotangent_ref[place, :], down)
+        share = 0.5 * lax.erf(linear * math.sqrt(0.5)) + 0.5
+        density = jnp.exp(linear * linear * -0.5) * (1.0 / math.sqrt(2.0 * math.pi))
+        hidden_ref[place, :] = (linear * share).astype(BF16)
+        low = (back * (share + linear * density)).astype(BF16)
+        back_ref[place, :] = low
+        total += jnp.sum(low.astype(F32), axis=0, keepdims=True)
+    sum_ref[...] += total
+
+
+def feed_forward(second_input, cotangent, up_full, down_full, up_bias):
+    count, width = second_input.shape[0], up_bias.shape[0]
+    high, wide = min(512, count), min(512, width)
+    rows_spec = pl.BlockSpec((high, D), lambda c, r: (r, 0))
+    weight_spec = pl.BlockSpec((D, wide), lambda c, r: (0, c))
+    line_spec = pl.BlockSpec((1, wide), lambda c, r: (0, c))
+    out_spec = pl.BlockSpec((high, wide), lambda c, r: (r, c))
+    return pl.pallas_call(
+        feed_forward_kernel,
+        grid=(width // wide, count // high),
+        in_specs=[rows_spec, rows_spec, weight_spec, weight_spec, line_spec],
+        out_specs=[out_spec, out_spec, line_spec],
+        out_shape=[
+            jax.ShapeDtypeStruct((count, width), BF16),
+            jax.ShapeDtypeStruct((count, width), BF16),
+            jax.ShapeDtypeStruct((1, width), F32),
+        ],
+        compiler_params=pltpu.CompilerParams(vmem_limit_bytes=32 << 20),
+        cost_estimate=pl.CostEstimate(
+            flops=4 * count * width * D,
+            bytes_accessed=4 * count * (width + D) + 4 * width * D,
+            transcendentals=2 * count * width,
+        ),
+        name="feed_forward",
+    )(second_input, cotangent, up_full, down_full, up_bias[None])
+
+
 def on_device(row, col, here, there):
     same = (lax.axis_index("rows") == row) & (lax.axis_index("cols") == col)
     pl.when(same)(here)
@@ -178,20 +224,39 @@
     lax.fori_loop(0, rows * cols, one, 0)
 
 
-def collect_kernel(
-    widths, rows, cols, from_ref, vector_ref, to_ref, pieces_ref,
-    send, take, cross_send, cross_take, piece_send, piece_take,
+def halves(value):
+    high = value.astype(BF16)
+    return high, (value - high.astype(F32)).astype(BF16)
+
+
+def muon_kernel(
+    widths, rows, cols, from_ref, vector_ref, to_ref, totals_ref,
+    matrix, grams, polys, gram_own, poly_own, turned, product, update, shrink, pieces, piece,
+    send, take, cross_send, cross_take, gram_send, gram_take, poly_send, poly_take,
+    spread_send, spread_take, piece_send, piece_take, total_send, total_take,
 ):
     row, col = lax.axis_index("rows"), lax.axis_index("cols")
+    core = lax.rem(row, 2)
     half_rows = rows // 2
-    depth = from_ref.shape[0]
-    half_depth = depth * half_rows
+    depth = to_ref.shape[0]
+    half = D // 2
+    step = ROWS_STEP
+    steps = half // step
+    me = row * cols + col
+
+    def roles(action):
+        start = 0
+        for place, width in enumerate(widths):
+            chip, plane = OWNERS[place]
+            pl.when((row // 2 == chip) & (col == plane))(partial(action, width, start))
+            start += width
+
     start = 0
     for place, width in enumerate(widths):
         chip, plane = OWNERS[place]
         target = 2 * chip + row // half_rows
         source = from_ref.at[:, pl.ds(start, width)]
-        goal = to_ref.at[pl.ds(row * depth, depth), pl.ds(col * width, width)]
+        goal = matrix.at[pl.ds(row * depth, depth), pl.ds(col * width, width)]
 
         def here(source=source, goal=goal):
             pltpu.make_async_copy(source, goal, take).start()
@@ -203,28 +268,203 @@
 
         on_device(target, plane, here, there)
         start += width
-    me = row * cols + col
-    to_all(rows, cols, lambda place: vector_ref.at[place], pieces_ref.at[me], piece_send, piece_take)
-    for place, width in enumerate(widths):
-        chip, plane = OWNERS[place]
-        core = lax.rem(row, 2)
-
-        @pl.when((row // 2 == chip) & (col == plane))
-        def _(width=width, core=core, plane=plane):
-            own = to_ref.at[pl.ds(core * half_depth, half_depth), pl.ds(0, cols * width)]
-            pltpu.make_async_copy(own, own, take).wait()
-            swap = pltpu.make_async_remote_copy(
-                own,
-                own,
-                cross_send,
-                cross_take,
-                device_id=(row + 1 - 2 * core, plane),
-                device_id_type=MESH,
-            )
-            swap.start()
-            other = to_ref.at[pl.ds((1 - core) * half_depth, half_depth), pl.ds(0, cols * width)]
-            swap.wait_send()
-            pltpu.make_async_copy(other, other, cross_take).wait()
+    to_all(rows, cols, lambda place: vector_ref.at[place], pieces.at[me], piece_send, piece_take)
+    pltpu.make_async_copy(pieces, pieces, piece_take).wait()
+    piece[...] = jnp.sum(pieces[...], axis=0)
+    to_all(rows, cols, lambda place: piece, totals_ref.at[me], total_send, total_take)
+
+    def own_rows(size, offset=0):
+        return pl.ds(pl.multiple_of(core * half + offset, size), size)
+
+    def other_rows(size):
+        return pl.ds(pl.multiple_of((1 - core) * half, size), size)
+
+    def cross(ref, send_sem, take_sem):
+        return pltpu.make_async_remote_copy(
+            ref, ref, send_sem, take_sem, device_id=(row + 1 - 2 * core, col), device_id_type=MESH
+        )
+
+    def gather_halves(width, start):
+        own = matrix.at[own_rows(half), pl.ds(0, cols * width)]
+        other = matrix.at[other_rows(half), pl.ds(0, cols * width)]
+        pltpu.make_async_copy(own, own, take).wait()
+        cross(own, cross_send, cross_take).start()
+        pltpu.make_async_copy(own, own, cross_send).wait()
+        pltpu.make_async_copy(other, other, cross_take).wait()
+
+    roles(gather_halves)
+    is_owner, columns = False, jnp.int32(1)
+    for (chip, plane), width in zip(OWNERS, widths):
+        own = (row // 2 == chip) & (col == plane)
+        is_owner = is_owner | own
+        columns = jnp.where(own, cols * width // D, columns)
+
+    def over_steps(body):
+        def one(number, carry):
+            body(pl.ds(pl.multiple_of(number * step, step), step), number * step)
+            return carry
+
+        lax.fori_loop(0, steps, one, 0)
+
+    def precise(left, right):
+        high, rest = halves(left)
+        return low_product(high, right[0]) + low_product(high, right[1]) + low_product(rest, right[0])
+
+    def share(value, ref, offset, send_sem, take_sem):
+        high, rest = halves(value)
+        place = own_rows(step, offset)
+        ref[0, place, :] = high
+        ref[1, place, :] = rest
+        cross(ref.at[:, place, :], send_sem, take_sem).start()
+
+    def shared(ref, send_sem, take_sem):
+        own, other = ref.at[:, own_rows(half), :], ref.at[:, other_rows(half), :]
+        pltpu.make_async_copy(own, own, send_sem).wait()
+        pltpu.make_async_copy(other, other, take_sem).wait()
+
+    @pl.when(is_owner)
+    def _():
+        def squares(number, total):
+            part = number // columns
+            block = matrix[
+                pl.ds(pl.multiple_of(part * step, step), step),
+                pl.ds(pl.multiple_of(lax.rem(number, columns) * D, D), D),
+            ].astype(F32)
+            return total + jnp.sum(block * block, axis=0, keepdims=True)
+
+        total = lax.fori_loop(0, columns * (D // step), squares, jnp.zeros((1, D), F32))
+        total = jnp.sum(total, axis=1, keepdims=True)
+        shrink[...] = jnp.broadcast_to(1.0 / (jnp.sqrt(total) + NORM_FLOOR), shrink.shape)
+        factor = shrink[0:1, 0:1]
+
+        def first_gram(place, offset):
+            gram_own[place, :] = jnp.zeros((step, D), F32)
+
+            def block(number, carry):
+                across = pl.ds(pl.multiple_of(number * D, D), D)
+                gram_own[place, :] += times_transpose(
+                    matrix[own_rows(step, offset), across], matrix[:, across]
+                )
+                return carry
+
+            lax.fori_loop(0, columns, block, 0)
+            value = (gram_own[place, :] * factor) * factor
+            gram_own[place, :] = value
+            share(value, grams.at[0], offset, gram_send.at[0], gram_take.at[0])
+
+        over_steps(first_gram)
+        shared(grams.at[0], gram_send.at[0], gram_take.at[0])
+
+        def iteration(number, carry):
+            now = lax.rem(number, 2)
+            later = 1 - now
+            gram, poly = grams.at[now], polys.at[now]
+
+            def make_poly(place, offset):
+                own = gram_own[place, :]
+                value = COEF_SECOND * own + COEF_THIRD * precise(own, gram)
+                poly_own[place, :] = value
+                share(value, poly, offset, poly_send.at[now], poly_take.at[now])
+
+            over_steps(make_poly)
+
+            @pl.when(number < ITERS - 1)
+            def _():
+                def turn(place, offset):
+                    turned[place, :] = COEF_FIRST * gram_own[place, :] + precise(
+                        poly_own[place, :], gram
+                    )
+
+                over_steps(turn)
+
+            @pl.when(number == 0)
+            def _():
+                def begin(place, offset):
+                    unit = (
+                        lax.broadcasted_iota(jnp.int32, (step, D), 0) + (core * half + offset)
+                        == lax.broadcasted_iota(jnp.int32, (step, D), 1)
+                    )
+                    product[place, :] = poly_own[place, :] + jnp.where(unit, COEF_FIRST, 0.0)
+
+                over_steps(begin)
+
+            shared(poly, poly_send.at[now], poly_take.at[now])
+
+            @pl.when(number < ITERS - 1)
+            def _():
+                def next_gram(place, offset):
+                    own = turned[place, :]
+                    value = COEF_FIRST * own + precise(own, poly)
+                    gram_own[place, :] = value
+                    share(value, grams.at[later], offset, gram_send.at[later], gram_take.at[later])
+
+                over_steps(next_gram)
+
+            @pl.when(number > 0)
+            def _():
+                def multiply(place, offset):
+                    own = product[place, :]
+                    product[place, :] = COEF_FIRST * own + precise(own, poly)
+
+                over_steps(multiply)
+
+            @pl.when(number < ITERS - 1)
+            def _():
+                shared(grams.at[later], gram_send.at[later], gram_take.at[later])
+
+            return carry
+
+        lax.fori_loop(0, ITERS, iteration, 0)
+
+    piece_rows = 128
+    near_count = piece_rows // depth
+
+    def finish(number, carry):
+        place = pl.ds(pl.multiple_of(number * piece_rows, piece_rows), piece_rows)
+
+        @pl.when(is_owner)
+        def _():
+            high, rest = halves(product[place, :] * shrink[0:1, 0:1])
+
+            def block(across, inner):
+                across = pl.ds(pl.multiple_of(across * D, D), D)
+                right = matrix[:, across]
+                update[place, across] = (low_product(high, right) + low_product(rest, right)).astype(
+                    BF16
+                )
+                return inner
+
+            lax.fori_loop(0, columns, block, 0)
+
+        def deliver(width, start):
+            def one(index, inner):
+                near, to_col = number * near_count + index // cols, lax.rem(index, cols)
+                to_row = core * half_rows + near
+                source = update.at[pl.ds(near * depth, depth), pl.ds(to_col * width, width)]
+                goal = to_ref.at[:, pl.ds(start, width)]
+
+                def here():
+                    pltpu.make_async_copy(source, goal, spread_take).start()
+
+                def there():
+                    pltpu.make_async_remote_copy(
+                        source,
+                        goal,
+                        spread_send,
+                        spread_take,
+                        device_id=(to_row, to_col),
+                        device_id_type=MESH,
+                    ).start()
+
+                on_device(to_row, to_col, here, there)
+                return inner
+
+            lax.fori_loop(0, near_count * cols, one, 0)
+
+        roles(deliver)
+        return carry
+
+    lax.fori_loop(0, half // piece_rows, finish, 0)
 
     start = 0
     for place, width in enumerate(widths):
@@ -236,191 +476,66 @@
 
         on_device(2 * chip + row // half_rows, plane, lambda: None, sent)
         start += width
-    pltpu.make_async_copy(pieces_ref, pieces_ref, piece_take).wait()
     others = vector_ref.at[pl.ds(0, rows * cols - 1)]
     pltpu.make_async_copy(others, others, piece_send).wait()
-
-
-def collect(moments, vector, widths, rows, cols):
-    depth = moments.shape[0]
-    return pl.pallas_call(
-        partial(collect_kernel, widths, rows, cols),
+    pltpu.make_async_copy(others, others, total_send).wait()
+    pltpu.make_async_copy(totals_ref, totals_ref, total_take).wait()
+    pltpu.make_async_copy(to_ref, to_ref, spread_take).wait()
+
+    def delivered(width, start):
+        def one(number, carry):
+            near, to_col = number // cols, lax.rem(number, cols)
+            source = update.at[pl.ds(near * depth, depth), pl.ds(to_col * width, width)]
+
+            def done():
+                pltpu.make_async_copy(source, source, spread_send).wait()
+
+            on_device(core * half_rows + near, to_col, lambda: None, done)
+            return carry
+
+        lax.fori_loop(0, half_rows * cols, one, 0)
+
+    roles(delivered)
+
+
+def orthogonalize(moments, vector, widths, rows, cols):
+    size, devices = vector.shape[0], rows * cols
+    lines = -(-size // (devices * 1024)) * 8
+    vector = jnp.pad(vector, (0, devices * lines * 128 - size)).reshape(devices, lines, 128)
+    half = D // 2
+    dma = pltpu.SemaphoreType.DMA
+    update, totals = pl.pallas_call(
+        partial(muon_kernel, widths, rows, cols),
         in_specs=[pl.BlockSpec(memory_space=pl.ANY)] * 2,
         out_specs=[pl.BlockSpec(memory_space=pl.ANY)] * 2,
         out_shape=[
-            jax.ShapeDtypeStruct((depth * rows, cols * max(widths)), BF16),
+            jax.ShapeDtypeStruct(moments.shape, BF16),
             jax.ShapeDtypeStruct(vector.shape, F32),
         ],
-        scratch_shapes=[pltpu.SemaphoreType.DMA((6,))] + [pltpu.SemaphoreType.DMA] * 5,
-        compiler_params=pltpu.CompilerParams(has_side_effects=True),
-        name="collect",
+        scratch_shapes=[
+            pltpu.VMEM((D, cols * max(widths)), BF16),
+            pltpu.VMEM((2, 2, D, D), BF16),
+            pltpu.VMEM((2, 2, D, D), BF16),
+            pltpu.VMEM((half, D), F32),
+            pltpu.VMEM((half, D), F32),
+            pltpu.VMEM((half, D), F32),
+            pltpu.VMEM((half, D), F32),
+            pltpu.VMEM((half, cols * max(widths)), BF16),
+            pltpu.VMEM((8, 128), F32),
+            pltpu.VMEM(vector.shape, F32),
+            pltpu.VMEM((lines, 128), F32),
+            dma((6,)), dma, dma, dma, dma((2,)), dma((2,)), dma((2,)), dma((2,)),
+            dma, dma, dma, dma, dma, dma,
+        ],
+        compiler_params=pltpu.CompilerParams(
+            has_side_effects=True, vmem_limit_bytes=56 << 20
+        ),
+        name="muon",
     )(moments, vector)
-
-
-def spread_kernel(
-    widths, rows, cols, from_ref, piece_ref, to_ref, pieces_ref, send, take, piece_send, piece_take
-):
-    row, col = lax.axis_index("rows"), lax.axis_index("cols")
-    half_rows = rows // 2
-    depth = to_ref.shape[0]
-    core = lax.rem(row, 2)
-    start = 0
-    for place, width in enumerate(widths):
-        chip, plane = OWNERS[place]
-
-        @pl.when((row // 2 == chip) & (col == plane))
-        def _(width=width, start=start):
-            def one(number, carry):
-                near, to_col = number // cols, lax.rem(number, cols)
-                to_row = core * half_rows + near
-                source = from_ref.at[pl.ds(near * depth, depth), pl.ds(to_col * width, width)]
-                goal = to_ref.at[:, pl.ds(start, width)]
-
-                def here():
-                    pltpu.make_async_copy(source, goal, take).start()
-
-                def there():
-                    pltpu.make_async_remote_copy(
-                        source, goal, send, take, device_id=(to_row, to_col), device_id_type=MESH
-                    ).start()
-
-                on_device(to_row, to_col, here, there)
-                return carry
-
-            lax.fori_loop(0, half_rows * cols, one, 0)
-
-        start += width
-    goal = pieces_ref.at[row * cols + col]
-    to_all(rows, cols, lambda place: piece_ref, goal, piece_send, piece_take)
-    pltpu.make_async_copy(to_ref, to_ref, take).wait()
-    for place, width in enumerate(widths):
-        chip, plane = OWNERS[place]
-
-        @pl.when((row // 2 == chip) & (col == plane))
-        def _(width=width):
-            def one(number, carry):
-                near, to_col = number // cols, lax.rem(number, cols)
-                source = from_ref.at[pl.ds(near * depth, depth), pl.ds(to_col * width, width)]
-
-                def sent():
-                    pltpu.make_async_copy(source, source, send).wait()
-
-                on_device(core * half_rows + near, to_col, lambda: None, sent)
-                return carry
-
-            lax.fori_loop(0, half_rows * cols, one, 0)
-
-    pltpu.make_async_copy(pieces_ref, pieces_ref, piece_take).wait()
-    others = pieces_ref.at[pl.ds(0, rows * cols - 1)]
-    pltpu.make_async_copy(others, others, piece_send).wait()
-
-
-def spread(update, piece, widths, rows, cols):
-    depth = D // rows
-    return pl.pallas_call(
-        partial(spread_kernel, widths, rows, cols),
-        in_specs=[pl.BlockSpec(memory_space=pl.ANY)] * 2,
-        out_specs=[pl.BlockSpec(memory_space=pl.ANY)] * 2,
-        out_shape=[
-            jax.ShapeDtypeStruct((depth, sum(widths)), BF16),
-            jax.ShapeDtypeStruct((rows * cols,) + piece.shape, F32),
-        ],
-        scratch_shapes=[pltpu.SemaphoreType.DMA] * 4,
-        compiler_params=pltpu.CompilerParams(has_side_effects=True),
-        name="spread",
-    )(update, piece)
-
-
-def swap_kernel(part_ref, whole_ref, send, take):
-    row, col = lax.axis_index("rows"), lax.axis_index("cols")
-    depth = part_ref.shape[0]
-    core = lax.rem(row, 2)
-    mine = whole_ref.at[pl.ds(pl.multiple_of(core * depth, depth), depth), :]
-    copy = pltpu.make_async_remote_copy(
-        part_ref, mine, send, take, device_id=(row + 1 - 2 * core, col), device_id_type=MESH
-    )
-    copy.start()
-    whole_ref[pl.ds(pl.multiple_of(core * depth, depth), depth), :] = part_ref[...]
-    copy.wait()
-
-
-def swap(part):
-    depth, width = part.shape
-    return pl.pallas_call(
-        swap_kernel,
-        in_specs=[pl.BlockSpec(memory_space=pltpu.VMEM)],
-        out_specs=pl.BlockSpec(memory_space=pltpu.VMEM),
-        out_shape=jax.ShapeDtypeStruct((2 * depth, width), part.dtype),
-        scratch_shapes=[pltpu.SemaphoreType.DMA, pltpu.SemaphoreType.DMA],
-        compiler_params=pltpu.CompilerParams(has_side_effects=True),
-        name="swap",
-    )(part)
-
-
-def orthogonalize(moments, vector, widths, rows, cols):
-    size = vector.shape[0]
-    lines = -(-size // (rows * cols * 128))
-    vector = jnp.pad(vector, (0, rows * cols * lines * 128 - size))
-    row, col = lax.axis_index("rows"), lax.axis_index("cols")
-    core = row % 2
-    half = D // 2
-    collected, pieces = collect(
-        moments, vector.reshape(rows * cols, lines, 128), widths, rows, cols
-    )
-    own_width = jnp.int32(0)
-    for (chip, plane), width in zip(OWNERS, widths):
-        own_width = jnp.where((row // 2 == chip) & (col == plane), cols * width, own_width)
-    kept = lax.broadcasted_iota(jnp.int32, collected.shape, 1) < own_width
-    matrix = jnp.where(kept, collected, jnp.zeros_like(collected))
-    part = times_transpose(lax.dynamic_slice_in_dim(matrix, core * half, half), matrix)
-    whole = swap(part)
-    place = lax.broadcasted_iota(jnp.int32, whole.shape, 0) == lax.broadcasted_iota(
-        jnp.int32, whole.shape, 1
-    )
-    total = jnp.sum(jnp.where(place, whole, 0.0))
-    shrink = 1.0 / (jnp.sqrt(total) + NORM_FLOOR)
-    gram = (whole * shrink) * shrink
-    part = (part * shrink) * shrink
-    unit = (
-        lax.broadcasted_iota(jnp.int32, part.shape, 0) + core * half
-        == lax.broadcasted_iota(jnp.int32, part.shape, 1)
-    ).astype(F32)
-    product = None
-    for step in range(ITERS):
-        final = step == ITERS - 1
-        if product is None:
-            first = three_pass(part, gram)
-            changed = COEF_FIRST * part + COEF_SECOND * first + COEF_THIRD * three_pass(first, gram)
-            product = COEF_FIRST * unit + COEF_SECOND * part + COEF_THIRD * first
-        elif final:
-            first = three_pass(product, gram)
-            product = (
-                COEF_FIRST * product + COEF_SECOND * first + COEF_THIRD * three_pass(first, gram)
-            )
-        else:
-            both = jnp.concatenate([part, product], axis=0)
-            first = three_pass(both, gram)
-            both = COEF_FIRST * both + COEF_SECOND * first + COEF_THIRD * three_pass(first, gram)
-            changed, product = both[:half], both[half:]
-        if not final:
-            first = three_pass(changed, gram)
-            part = (
-                COEF_FIRST * changed + COEF_SECOND * first + COEF_THIRD * three_pass(first, gram)
-            )
-            gram = swap(part)
-    high = product.astype(BF16)
-    rest = (product - high.astype(F32)).astype(BF16)
-    update = (low_product(high, matrix) + low_product(rest, matrix)) * shrink
-    update, total = spread(update.astype(BF16), jnp.sum(pieces, 0), widths, rows, cols)
-    return update, total.reshape(-1)[:size]
+    return update, totals.reshape(-1)[:size]
 
 
 def split_sum(part_of, cols):
-    col = lax.axis_index("cols")
-    if cols == 2:
-        sent = part_of(1 - col).astype(BF16)
-        taken = lax.ppermute(sent, "cols", [(0, 1), (1, 0)])
-        return part_of(col) + taken.astype(F32)
     parts = jnp.concatenate([part_of(place) for place in range(cols)], axis=1)
     return lax.psum_scatter(parts, "cols", scatter_dimension=1, tiled=True)
 
@@ -503,28 +618,31 @@
     normed = centered * inverse_scale
     first_input = (normed * first_gain + first_shift).astype(BF16)
     second_input = (normed * second_gain + second_shift).astype(BF16)
-    up_linear = low_product(second_input, up_full) + up_bias
-    activation, activation_back = jax.vjp(partial(jax.nn.gelu, approximate=False), up_linear)
-    hidden = activation.astype(BF16)
-    hidden_back = low_product(whole_cotangent, down_full)
-    up_back = activation_back(hidden_back)[0].astype(BF16)
+    hidden, up_back, up_sum = feed_forward(
+        second_input, whole_cotangent, up_full, down_full, up_bias
+    )
 
     def reduced(part):
-        return lax.psum_scatter(part, "rows", scatter_dimension=0, tiled=True)
+        return lax.psum_scatter(part, "rows", scatter_dimension=0, tiled=True).astype(F32)
 
     down_part, up_part = inner_rows(whole_cotangent, hidden), inner_rows(second_input, up_back)
-    down_part, up_part, first_input = lax.optimization_barrier((down_part, up_part, first_input))
-    down_sums, up_sums = reduced(down_part), reduced(up_part)
+    down_part, up_part, first_input, late_cotangent = lax.optimization_barrier(
+        (down_part, up_part, first_input, whole_cotangent)
+    )
+    down_sums, up_sums = reduced(down_part.astype(BF16)), reduced(up_part.astype(BF16))
     linear_bias = jnp.concatenate([query_bias, jnp.zeros_like(query_bias), value_bias])
     projected = low_product(first_input, projection) + linear_bias
-    attended_back = low_product(whole_cotangent, output_full).astype(BF16)
+    attended_back = low_product(late_cotangent, output_full).astype(BF16)
     attended_low, query_back, key_back, value_back = attention(
         projected, attended_back, rotary_tables()
     )
 
+    attended_low, query_back, key_back, value_back, down_sums = lax.optimization_barrier(
+        (attended_low, query_back, key_back, value_back, down_sums)
+    )
     projected_back = jnp.concatenate([query_back, key_back, value_back], axis=1)
     other_part = jnp.concatenate(
-        [inner_rows(first_input, projected_back), inner_rows(whole_cotangent, attended_low)], axis=1
+        [inner_rows(first_input, projected_back), inner_rows(late_cotangent, attended_low)], axis=1
     )
     other_part, attended_low, projected_back = lax.optimization_barrier(
         (other_part, attended_low, projected_back)
@@ -536,8 +654,13 @@
         down_part = lax.dynamic_slice_in_dim(down_full, place * local_width, local_width)
         return times_transpose(attended_low, output_part) + times_transpose(hidden, down_part)
 
-    branch_share = split_sum(branch_part, cols)
-    result = (tokens.astype(F32) + branch_share + out_bias).astype(BF16)
+    if cols == 2:
+        sent = branch_part(1 - col).astype(BF16)
+        sent, projected_back, up_sums = lax.optimization_barrier((sent, projected_back, up_sums))
+        branch_taken = lax.ppermute(sent, "cols", [(0, 1), (1, 0)])
+        branch_own = branch_part(col)
+    else:
+        branch_taken, branch_own = jnp.zeros((), BF16), split_sum(branch_part, cols)
     first_back = times_transpose(projected_back, projection)
     second_back = times_transpose(up_back, up_full)
     norm_partials = jnp.stack(
@@ -552,10 +675,18 @@
     row_sums = full_sum(
         jnp.stack([jnp.sum(normed_part, 1), jnp.sum(normed_part * normed, 1)]), cols
     )
-    normed_back = split_sum(
-        lambda place: lax.dynamic_slice_in_dim(normed_part, place * local_width, local_width, 1),
-        cols,
-    )
+    def normed_place(place):
+        return lax.dynamic_slice_in_dim(normed_part, place * local_width, local_width, 1)
+
+    if cols == 2:
+        sent, branch_taken = lax.optimization_barrier(
+            (normed_place(1 - col).astype(BF16), branch_taken)
+        )
+        taken = lax.ppermute(sent, "cols", [(0, 1), (1, 0)])
+        normed_back = normed_place(col) + taken.astype(F32)
+    else:
+        normed_back = split_sum(normed_place, cols)
+    result = (tokens.astype(F32) + branch_own + branch_taken.astype(F32) + out_bias).astype(BF16)
     own_normed = (tokens.astype(F32) - mean_value) * inverse_scale
     back_mean = (row_sums[0] / D)[:, None]
     cross_mean = (row_sums[1] / D)[:, None]
@@ -573,7 +704,7 @@
         [
             jnp.sum(query_back, 0, dtype=F32),
             jnp.sum(value_back, 0, dtype=F32),
-            jnp.sum(up_back, 0, dtype=F32),
+            up_sum[0],
             jnp.sum(cotangent, 0, dtype=F32),
         ]
     )

time: 1030 us -> 658 us (0.64)
  matrix products: 331 us -> 107 us
  waiting for transfers between devices: 336 us -> 144 us
  Pallas kernels: 251 us -> 291 us
  local copies, waits for them, and re-layouts: 23 us -> 36.4 us
    reduce_scatter x3, waiting for transfers between devices: 177 us -> 18.7 us  [reduced(): lax.psum_scatter(part, 'rows', scatter_dimension=0, tiled=True).astype(F32)]
    dot_general x18 -> x0, matrix products: 109 us -> none  [three_pass(): return jnp.dot(left, right, precision=lax.Precision.HIGH)]
    dot_general x6 -> x2, matrix products: 111 us -> 16.3 us  [low_product(): return jnp.dot(left, right, preferred_element_type=F32)]
    pallas_call x7 -> x2, Pallas kernels: 180 us -> 219 us  [the longest x1 194 us: orthogonalize(): pl.pallas_call(partial(muon_kernel, widths, rows, cols), in_specs=[pl.Blo...]
    ppermute x2, waiting for transfers between devices: 40.3 us -> 12.2 us  [the longest x1 12.2 us: shards(): branch_taken = lax.ppermute(sent, 'cols', [(0, 1), (1, 0)])]
    all_gather x1, waiting for transfers between devices: 19.2 us -> 0.01 us  [shards(): forward_full = lax.all_gather(forward_low, 'rows', axis=0, tiled=True)]
    dot_general x7 -> x6, matrix products: 67.3 us -> 51.7 us  [times_transpose(): lax.dot_general(left, right, (((1,), (1,)), ((), ())), preferred_element_...]
    unnamed x145 -> x137, local copies, waits for them, and re-layouts: 4.77 us -> 19.2 us
  transfers between devices with their start and end apart: 10 -> 10, of which waited for: 7 -> 5; matrix products, arithmetic and copies ran while one was open for 10% -> 24% of each run, Pallas kernels for 0% -> 15%
where the time goes in v2:
time: 658 us; the launch traced here: 650 us
  Pallas kernels  291 us (44%)
  waiting for transfers between devices  144 us (22%)
  matrix products  107 us (16%)
  other arithmetic  52.1 us (8%)
  local copies, waits for them, and re-layouts  36.4 us (6%)
  between operations  15 us (2%)
    pallas_call x1, Pallas kernels, orthogonalize(): pl.pallas_call(partial(muon_kernel, widths, rows, cols), in_specs=[pl.Blo...  194 us
    ppermute x2, waiting for transfers between devices, whole_width(): taken = lax.ppermute(own, 'cols', [(0, 1), (1, 0)])  79.3 us
    pallas_call x1, Pallas kernels, attention(): pl.pallas_call(attention_kernel, grid=(rows // LEN, pairs), in_specs=[pla...  72.3 us
    dot_general x6, matrix products, times_transpose(): lax.dot_general(left, right, (((1,), (1,)), ((), ())), preferred_element_...  51.7 us
    dot_general x4, matrix products, inner_rows(): lax.dot_general(left, right, (((0,), (0,)), ((), ())), preferred_element_...  38.9 us
    ppermute x1, waiting for transfers between devices, full_sum(): return value + lax.ppermute(value, 'cols', [(0, 1), (1, 0)])  34.2 us
    pallas_call x1, Pallas kernels, feed_forward(): pl.pallas_call(feed_forward_kernel, grid=(width // wide, count // high),...  25.2 us
    unnamed x137, local copies, waits for them, and re-layouts  19.2 us
  transfers between devices with their start and end apart: 10, of which 5 were waited for; matrix products, arithmetic and copies ran while one was open for 24% of the time, Pallas kernels for 15%

profile of v2, /device:TPU:15, one launch (start us, length us, event | category | flops | bytes accessed | tf_op | source)
XLA Modules:
  0.0 649.6 jit_solution(8498186211611672568)
XLA Ops:
  19.0 38.4 %collective-permute-done.1 = bf16[2048,512]{1,0:T(8,128)(2,1)} collective-permute-done((bf16[2048,512]{1,0:T(8,128)(2,1)}, bf16[2048,512]{1,0:T(8,128)(2,1)}, u32[]{:S(2)}, u32[]{:S(2)}) %collective-permute-start.1) | collective-permute-done | bytes 2097184 | tf_op jit(solution)/shard_map/ppermute | solution.py:546
  57.4 1.9 constant_dynamic-update-slice_fusion.3
  61.4 40.9 %collective-permute-done = bf16[2048,512]{1,0:T(8,128)(2,1)} collective-permute-done((bf16[2048,512]{1,0:T(8,128)(2,1)}, bf16[2048,512]{1,0:T(8,128)(2,1)}, u32[]{:S(2)}, u32[]{:S(2)}) %collective-permute-start) | collective-permute-done | bytes 2097184 | tf_op jit(solution)/shard_map/ppermute | solution.py:546
  102.3 1.9 constant_dynamic-update-slice_fusion.5.cotangent_ref
  104.3 2.0 copy-done
  106.3 4.4 fusion.10
  110.7 4.2 fusion.58
  115.6 2.9 copy-done.9
  118.6 25.2 %feed_forward.1 = (bf16[2048,2048]{1,0:T(8,128)(2,1)}, bf16[2048,2048]{1,0:T(8,128)(2,1)}, f32[1,2048]{1,0:T(1,128)S(1)}) custom-call(bf16[2048,1024]{1,0:T(8,128)(2,1)S(1)} %copy-done.9, bf16[2048,1024]{1,0:T(8,128)(2,1)S(1)} %copy-done.1, bf16[1024,2048]{1,0:T(8,128)(2,1)S(1)} %get-tuple-element.144.up_ref, ...), custom_call_target="tpu_custom_call" | custom-call | flops 17179869184 | bytes 33554432 | tf_op jit(solution)/shard_map/feed_forward/pallas_call | solution.py:180
  143.7 13.1 %fusion.61 = bf16[1024,2048]{1,0:T(8,128)(2,1)} fusion(bf16[2048,1024]{1,0:T(8,128)(2,1)S(1)} %copy-done.9, bf16[2048,2048]{1,0:T(8,128)(2,1)} %get-tuple-element.71), kind=kOutput, calls=%fused_computation.149 | convolution fusion | flops 8589934592 | bytes 16777216 | tf_op jit(solution)/shard_map/dot_general | solution.py:45
  156.8 14.2 %fusion.60 = bf16[1024,2048]{1,0:T(8,128)(2,1)} fusion(bf16[2048,1024]{1,0:T(8,128)(2,1)} %copy-done, bf16[2048,2048]{1,0:T(8,128)(2,1)} %get-tuple-element.70), kind=kOutput, calls=%fused_computation.148 | convolution fusion | flops 8589934592 | bytes 16777216 | tf_op jit(solution)/shard_map/dot_general | solution.py:45
  171.7 3.0 fusion.28
  174.7 2.3 slice.134
  177.1 12.6 %convolution_add_fusion.query_ref.key_ref.value_ref = f32[2048,1536]{1,0:T(8,128)} fusion(bf16[2048,1024]{1,0:T(8,128)(2,1)} %get-tuple-element.72, f32[1536]{0:T(1024)S(1)} %pad_maximum_fusion.5, bf16[1024,2048]{1,0:T(8,128)(2,1)} %all-gather.5.cloned.1.call-done), kind=kOutput, calls=%fused_computation.9 | convolution fusion | flops 6445596672 | bytes 19929088 | tf_op jit(solution)/shard_map/dot_general | solution.py:37
  189.7 3.7 convolution_convert_fusion.back_ref
  193.4 72.3 %attention.1 = (bf16[2048,512]{1,0:T(8,128)(2,1)S(1)}, bf16[2048,512]{1,0:T(8,128)(2,1)S(1)}, bf16[2048,512]{1,0:T(8,128)(2,1)S(1)}, bf16[2048,512]{1,0:T(8,128)(2,1)S(1)}) custom-call(f32[2048,1536]{1,0:T(8,128)} %convolution_add_fusion.query_ref.key_ref.value_ref, f32[2048,1536]{1,0:T(8,128)} %convolution_add_fusion.query_ref.key_ref.value_ref, ...), custom_call_target="tpu_custom_call" | custom-call | flops 12884901888 | bytes 23068672 | tf_op jit(solution)/shard_map/attention/pallas_call | solution.py:127
  269.7 1.9 convert_element_type.136
  275.8 2.4 fusion.63
  280.3 9.2 %fusion.62 = f32[1024,1536]{1,0:T(8,128)} fusion(bf16[2048,1024]{1,0:T(8,128)(2,1)S(1)} %copy-done.23, bf16[2048,1536]{1,0:T(8,128)(2,1)S(1)} %constant_dynamic-update-slice_fusion), kind=kOutput, calls=%fused_computation.150 | convolution fusion | flops 6442450944 | bytes 16777216 | tf_op jit(solution)/shard_map/dot_general | solution.py:45
  289.6 6.9 %pad_maximum_fusion = f32[1024,2048]{1,0:T(8,128)} fusion(f32[1024,512]{1,0:T(8,128)S(1)} %fusion.63, f32[1024,1536]{1,0:T(8,128)} %fusion.62), kind=kLoop, calls=%fused_computation.18 | loop fusion | flops 2097152 | bytes 16777216 | tf_op jit(solution)/shard_map/concatenate | solution.py:644
  297.7 3.3 fusion.34
  301.0 18.7 %reduce-scatter.6.cloned.1.call-done = bf16[64,2048]{1,0:T(8,128)(2,1)} async-done(((bf16[1024,2048]{1,0:T(8,128)(2,1)}), bf16[64,2048]{1,0:T(8,128)(2,1)}) %reduce-scatter.6.cloned.1.call-update) | async-done | bytes 262160 | tf_op jit(solution)/shard_map/reduce_scatter | solution.py:626
  319.6 1.9 convert_element_type.139
  321.6 11.3 %add_convert_fusion = bf16[2048,512]{1,0:T(8,128)(2,1)} fusion(f32[2048,512]{1,0:T(8,128)} %fusion.34, bf16[2048,2048]{1,0:T(8,128)(2,1)} %get-tuple-element.70, bf16[1024,2048]{1,0:T(8,128)(2,1)} %copy-done.10, s32[]{:T(128)S(6)} %select_n.64), kind=kOutput, calls=%fused_computation.34 | convolution fusion | flops 4297064448 | bytes 16777220 | tf_op jit(solution)/shard_map/dot_general | solution.py:41
  333.2 9.4 %fusion.22 = f32[2048,1024]{1,0:T(8,128)} fusion(bf16[2048,1536]{1,0:T(8,128)(2,1)S(1)} %bitcast.76, bf16[1024,2048]{1,0:T(8,128)(2,1)S(1)} %copy-done.37), kind=kOutput, calls=%fused_computation.36 | convolution fusion | flops 6442450944 | bytes 17825792 | tf_op jit(solution)/shard_map/dot_general | solution.py:41
  342.5 19.4 %fusion.57 = (f32[2048]{0:T(1024)S(1)}, f32[2048]{0:T(1024)S(1)}, f32[1024]{0:T(1024)S(1)}, f32[1024]{0:T(1024)S(1)}, f32[1024]{0:T(1024)S(1)}, /*index=5*/f32[1024]{0:T(1024)S(1)}, f32[2048,1024]{1,0:T(8,128)}) fusion(f32[2048]{0:T(1024)S(1)} %add_rsqrt_fusion, f32[2048]{0:T(1024)S(1)} %broadcast_multiply_fusion, bf16[2048,1024]{1,0:T(8,128)(2,1)S(1)} %copy-done.18, ...), kind=kOutput, calls=%fused_computation.145 | convolution fusion | flops 8621383680 | bytes 33611776 | tf_op jit(solution)/shard_map/dot_general | solution.py:41
  362.0 3.9 dynamic-slice_convert_fusion
  365.9 12.2 %collective-permute-done.2 = bf16[2048,512]{1,0:T(8,128)(2,1)S(1)} collective-permute-done((bf16[2048,512]{1,0:T(8,128)(2,1)}, bf16[2048,512]{1,0:T(8,128)(2,1)S(1)}, u32[]{:S(2)}, u32[]{:S(2)}) %collective-permute-start.2) | collective-permute-done | bytes 2097184 | tf_op jit(solution)/shard_map/ppermute | solution.py:660
  378.4 7.1 %fusion.26 = f32[2048,512]{1,0:T(8,128)S(1)} fusion(bf16[2048,2048]{1,0:T(8,128)(2,1)} %get-tuple-element.70, bf16[1024,2048]{1,0:T(8,128)(2,1)S(1)} %copy-done.11, s32[]{:T(128)S(6)} %select_n.63), kind=kOutput, calls=%fused_computation.40 | convolution fusion | flops 4294967296 | bytes 14680068 | tf_op jit(solution)/shard_map/dot_general | solution.py:41
  388.8 34.2 %collective-permute-done.4 = f32[2,2048]{1,0:T(2,128)S(1)} collective-permute-done((f32[2,2048]{1,0:T(2,128)S(1)}, f32[2,2048]{1,0:T(2,128)S(1)}, u32[]{:S(2)}, u32[]{:S(2)}) %collective-permute-start.4) | collective-permute-done | bytes 16416 | tf_op jit(solution)/shard_map/ppermute | solution.py:555
  423.2 6.3 convert_reduce_fusion.1
  439.6 193.8 %muon.1 = (bf16[64,6144]{1,0:T(8,128)(2,1)}, f32[32,8,128]{2,1,0:T(8,128)}) custom-call(bf16[64,6144]{1,0:T(8,128)(2,1)} %copy-done.29, f32[32,8,128]{2,1,0:T(8,128)} %fusion.43.vector_ref), custom_call_target="tpu_custom_call" | custom-call | tf_op jit(solution)/shard_map/muon/pallas_call | solution.py:507
  (212 shorter events, 49.6 us)
Async XLA Ops:
  7.2 103.5 %all-gather.3.cloned.1.call-start = ((), (), s32[]{:S(2)}) async-start(), calls=%async_computation.3 | async-start | bytes 8912896 | tf_op jit(solution)/shard_map/all_gather | solution.py:607
  10.4 164.3 %all-gather.5.cloned.1.call-start = ((), (), s32[]{:S(2)}) async-start(), calls=%async_computation.4 | async-start | bytes 4456448 | tf_op jit(solution)/shard_map/all_gather | solution.py:608
  10.5 46.9 %collective-permute-start.1 = (bf16[2048,512]{1,0:T(8,128)(2,1)}, bf16[2048,512]{1,0:T(8,128)(2,1)}, u32[]{:S(2)}, u32[]{:S(2)}) collective-permute-start(bf16[2048,512]{1,0:T(8,128)(2,1)} %param.30), channel_id=1, source_target_pairs={{0,1},{1,0},{2,3},{3,2},{4,5},{5,4},{6,7},{7,6},{8,9},{9,8},{10,11... | collective-permute-start | bytes 6291464 | tf_op jit(solution)/shard_map/ppermute | solution.py:546
  10.8 91.5 %collective-permute-start = (bf16[2048,512]{1,0:T(8,128)(2,1)}, bf16[2048,512]{1,0:T(8,128)(2,1)}, u32[]{:S(2)}, u32[]{:S(2)}) collective-permute-start(bf16[2048,512]{1,0:T(8,128)(2,1)} %param.31), channel_id=1, source_target_pairs={{0,1},{1,0},{2,3},{3,2},{4,5},{5,4},{6,7},{7,6},{8,9},{9,8},{10,11... | collective-permute-start | bytes 6291464 | tf_op jit(solution)/shard_map/ppermute | solution.py:546
  16.4 253.2 %reduce-scatter.4.cloned.1.call-start = ((), (), s32[]{:S(2)}) async-start(), calls=%async_computation.5 | async-start | bytes 4456448 | tf_op jit(solution)/shard_map/reduce_scatter | solution.py:626
  60.0 46.3 %copy-start.43 = (f32[1024]{0:T(1024)S(1)}, f32[1024]{0:T(1024)}, u32[]{:S(2)}) copy-start(f32[1024]{0:T(1024)} %param.33) | copy-start | bytes 12292
  60.0 46.3 %copy-start.45 = (f32[1024]{0:T(1024)S(1)}, f32[1024]{0:T(1024)}, u32[]{:S(2)}) copy-start(f32[1024]{0:T(1024)} %param.32) | copy-start | bytes 12292
  60.0 46.3 %copy-start.46 = (f32[1024]{0:T(1024)S(1)}, f32[1024]{0:T(1024)}, u32[]{:S(2)}) copy-start(f32[1024]{0:T(1024)} %param.35) | copy-start | bytes 12292
  171.0 148.6 %reduce-scatter.6.cloned.1.call-start = ((), (), s32[]{:S(2)}) async-start(), calls=%async_computation.6 | async-start | bytes 4456448 | tf_op jit(solution)/shard_map/reduce_scatter | solution.py:626
  177.0 253.3 %reduce-scatter.8.cloned.1.call-start = ((), (), s32[]{:S(2)}) async-start(), calls=%async_computation.7 | async-start | bytes 8912896 | tf_op jit(solution)/shard_map/reduce_scatter | solution.py:626
  332.9 45.3 %collective-permute-start.2 = (bf16[2048,512]{1,0:T(8,128)(2,1)}, bf16[2048,512]{1,0:T(8,128)(2,1)S(1)}, u32[]{:S(2)}, u32[]{:S(2)}) collective-permute-start(bf16[2048,512]{1,0:T(8,128)(2,1)} %add_convert_fusion), channel_id=1, source_target_pairs={{0,1},{1,0},{2,3},{3,2},{4,5},{5,4},{6,7},{7,6},{8,9},{9,8},{10,11... | collective-permute-start | bytes 6291464 | tf_op jit(solution)/shard_map/ppermute | solution.py:660
  362.0 61.1 %slice-start = ((s8[8388608]{0:T(1024)(128)(4,1)}), s8[4194304]{0:T(1024)(128)(4,1)S(1)}, s32[]{:S(2)}) async-start(s8[8388608]{0:T(1024)(128)(4,1)} %bitcast.72), calls=%async_computation.8 | async-start | bytes 8388608
  365.9 57.1 %slice-start.1 = ((s8[8388608]{0:T(1024)(128)(4,1)}), s8[4194304]{0:T(1024)(128)(4,1)S(1)}, s32[]{:S(2)}) async-start(s8[8388608]{0:T(1024)(128)(4,1)} %bitcast.72), calls=%async_computation.9 | async-start | bytes 8388608
  378.1 44.9 %collective-permute-start.3 = (bf16[2048,512]{1,0:T(8,128)(2,1)}, bf16[2048,512]{1,0:T(8,128)(2,1)}, u32[]{:S(2)}, u32[]{:S(2)}) collective-permute-start(bf16[2048,512]{1,0:T(8,128)(2,1)} %dynamic-slice_convert_fusion), channel_id=1, source_target_pairs={{0,1},{1,0},{2,3},{3,2},{4,5},{5,4},{6,7},{7,6},{8,9},{9,8},{10,11... | collective-permute-start | bytes 6291464 | tf_op jit(solution)/shard_map/ppermute | solution.py:685
  385.5 37.5 %collective-permute-start.4 = (f32[2,2048]{1,0:T(2,128)S(1)}, f32[2,2048]{1,0:T(2,128)S(1)}, u32[]{:S(2)}, u32[]{:S(2)}) collective-permute-start(f32[2,2048]{1,0:T(2,128)S(1)} %pad_maximum_fusion.3), channel_id=1, source_target_pairs={{0,1},{1,0},{2,3},{3,2},{4,5},{5,4},{6,7},{7,6},{8,9},{9,8},{10,11... | collective-permute-start | bytes 49160 | tf_op jit(solution)/shard_map/ppermute | solution.py:555
  433.6 201.1 %copy-start.33 = (f32[512,64]{0,1:T(8,128)S(1)}, f32[512,64]{0,1:T(8,128)}, u32[]{:S(2)}) copy-start(f32[512,64]{0,1:T(8,128)} %param.41) | copy-start | bytes 393220
  433.6 201.8 %copy-start.34 = (f32[64,512]{1,0:T(8,128)S(1)}, f32[64,512]{1,0:T(8,128)}, u32[]{:S(2)}) copy-start(f32[64,512]{1,0:T(8,128)} %param.38) | copy-start | bytes 393220
  433.6 201.8 %copy-start.35 = (f32[64,512]{1,0:T(8,128)S(1)}, f32[64,512]{1,0:T(8,128)}, u32[]{:S(2)}) copy-start(f32[64,512]{1,0:T(8,128)} %param.37) | copy-start | bytes 393220
  433.6 201.8 %copy-start.36 = (f32[64,512]{1,0:T(8,128)S(1)}, f32[64,512]{1,0:T(8,128)}, u32[]{:S(2)}) copy-start(f32[64,512]{1,0:T(8,128)} %param.36) | copy-start | bytes 393220
  435.3 200.8 %copy-start.25 = (f32[2048,64]{0,1:T(8,128)S(1)}, f32[2048,64]{0,1:T(8,128)}, u32[]{:S(2)}) copy-start(f32[2048,64]{0,1:T(8,128)} %param.44) | copy-start | bytes 1572868
  437.8 199.2 %copy-start.26 = (f32[64,2048]{1,0:T(8,128)S(1)}, f32[64,2048]{1,0:T(8,128)}, u32[]{:S(2)}) copy-start(f32[64,2048]{1,0:T(8,128)} %param.42) | copy-start | bytes 1572868
  438.7 200.1 %copy-start.60 = (f32[512]{0:T(512)S(1)}, f32[512]{0:T(512)}, u32[]{:S(2)}) copy-start(f32[512]{0:T(512)} %param.54) | copy-start | bytes 6148
  438.7 200.7 %copy-start.61 = (f32[512]{0:T(512)S(1)}, f32[512]{0:T(512)}, u32[]{:S(2)}) copy-start(f32[512]{0:T(512)} %param.59) | copy-start | bytes 6148
  438.7 201.3 %copy-start.62 = (f32[512]{0:T(512)S(1)}, f32[512]{0:T(512)}, u32[]{:S(2)}) copy-start(f32[512]{0:T(512)} %param.53) | copy-start | bytes 6148
  438.7 201.9 %copy-start.16 = (f32[2048]{0:T(1024)S(1)}, f32[2048]{0:T(1024)}, u32[]{:S(2)}) copy-start(f32[2048]{0:T(1024)} %param.43) | copy-start | bytes 24580
  438.7 201.9 %copy-start.50 = (f32[2048]{0:T(1024)S(1)}, f32[2048]{0:T(1024)}, u32[]{:S(2)}) copy-start(f32[2048]{0:T(1024)} %param.57) | copy-start | bytes 24580
  438.8 202.5 %copy-start.44 = (f32[1024]{0:T(1024)S(1)}, f32[1024]{0:T(1024)}, u32[]{:S(2)}) copy-start(f32[1024]{0:T(1024)} %param.33) | copy-start | bytes 12292
  438.8 202.5 %copy-start.47 = (f32[1024]{0:T(1024)S(1)}, f32[1024]{0:T(1024)}, u32[]{:S(2)}) copy-start(f32[1024]{0:T(1024)} %param.35) | copy-start | bytes 12292
  438.8 202.4 %copy-start.56 = (f32[1024]{0:T(1024)S(1)}, f32[1024]{0:T(1024)}, u32[]{:S(2)}) copy-start(f32[1024]{0:T(1024)} %param.49) | copy-start | bytes 12292
  438.8 202.4 %copy-start.57 = (f32[1024]{0:T(1024)S(1)}, f32[1024]{0:T(1024)}, u32[]{:S(2)}) copy-start(f32[1024]{0:T(1024)} %param.48) | copy-start | bytes 12292
  438.8 202.4 %copy-start.58 = (f32[1024]{0:T(1024)S(1)}, f32[1024]{0:T(1024)}, u32[]{:S(2)}) copy-start(f32[1024]{0:T(1024)} %param.47) | copy-start | bytes 12292
  438.8 202.4 %copy-start.59 = (f32[1024]{0:T(1024)S(1)}, f32[1024]{0:T(1024)}, u32[]{:S(2)}) copy-start(f32[1024]{0:T(1024)} %param.46) | copy-start | bytes 12292
  (45 other events, 496.7 us)
Sparse Core Ops, SparseCore 0:
  10.8 74.6 all-gather.2
  88.2 49.2 all-gather.4
  171.2 72.8 reduce-scatter.3
  247.8 71.8 reduce-scatter.5
  323.5 104.2 reduce-scatter.7
